TPU v7x, 8 devices: a whole 2x2x1 slice. The times are simulated.
8 devices in a mesh: stage: 2 (over z, y), data: 4 (over x, core).
Axes of the slice: x: 2, y: 2, z: 1, core: 2. Of those that a mesh axis runs over, the one named last changes fastest.
Arguments:
- grad_attn: float32 [8, 4, 448, 448], P(('stage', 'data')), parts along dimension 0
- grad_shared_in: float32 [8, 2, 448, 2560], P(('stage', 'data')), parts along dimension 0
- grad_shared_out: float32 [8, 1, 2560, 448], P(('stage', 'data')), parts along dimension 0
- grad_expert_in: float32 [8, 32, 448, 320], P(('stage', 'data')), parts along dimension 0
- grad_expert_out: float32 [8, 16, 320, 448], P(('stage', 'data')), parts along dimension 0
- mom_attn: float32 [8, 448, 448], P('stage', 'data'), parts along dimension 0
- mom_shared_in: float32 [4, 448, 2560], P('stage', 'data'), parts along dimension 0
- mom_shared_out: float32 [2, 2560, 448], P('stage', 'data'), parts along dimension 0
- mom_expert_in: float32 [64, 448, 320], P('stage', 'data'), parts along dimension 0
- mom_expert_out: float32 [32, 320, 448], P('stage', 'data'), parts along dimension 0
- master_attn: float32 [8, 448, 448], P('stage', 'data'), parts along dimension 0
- master_shared_in: float32 [4, 448, 2560], P('stage', 'data'), parts along dimension 0
- master_shared_out: float32 [2, 2560, 448], P('stage', 'data'), parts along dimension 0
- master_expert_in: float32 [64, 448, 320], P('stage', 'data'), parts along dimension 0
- master_expert_out: float32 [32, 320, 448], P('stage', 'data'), parts along dimension 0
Outputs:
- output 1: float32 [8, 448, 448], P('stage', 'data'), parts along dimension 0
- output 2: float32 [4, 448, 2560], P('stage', 'data'), parts along dimension 0
- output 3: float32 [2, 2560, 448], P('stage', 'data'), parts along dimension 0
- output 4: float32 [64, 448, 320], P('stage', 'data'), parts along dimension 0
- output 5: float32 [32, 320, 448], P('stage', 'data'), parts along dimension 0
- output 6: float32 [8, 448, 448], P('stage', 'data'), parts along dimension 0
- output 7: float32 [4, 448, 2560], P('stage', 'data'), parts along dimension 0
- output 8: float32 [2, 2560, 448], P('stage', 'data'), parts along dimension 0
- output 9: float32 [64, 448, 320], P('stage', 'data'), parts along dimension 0
- output 10: float32 [32, 320, 448], P('stage', 'data'), parts along dimension 0
- output 11: bfloat16 [8, 448, 448], P('stage'), parts along dimension 0
- output 12: bfloat16 [4, 448, 2560], P('stage'), parts along dimension 0
- output 13: bfloat16 [2, 2560, 448], P('stage'), parts along dimension 0
- output 14: bfloat16 [64, 448, 320], P('stage'), parts along dimension 0
- output 15: bfloat16 [32, 320, 448], P('stage'), parts along dimension 0
There are 2 independent parts. A program takes and returns all parts, laid end to end along the dimension named above; each array names one.
All inputs are finite; a program needn't handle non-finite values.
Results may differ from a plain program's by a relative error of at most 0.00507594.
Values are sent between devices in bfloat16 or wider.
A program may use at most 1 GiB of HBM per device.

v0:
```python
import math
import jax
import jax.numpy as jnp
from jax import lax
from jax.sharding import PartitionSpec as P

NS_STEPS = 5
MOMENTUM = 0.95
LEARN_RATE = 0.2
WEIGHT_DECAY = 0.25
NORM_EPS = 1e-7
COEF_A = 3.4445
COEF_B = -4.7750
COEF_C = 2.0315


def orthogonalize(mat_stack):
    is_tall = mat_stack.shape[1] > mat_stack.shape[2]
    iterate = mat_stack
    for iteration in range(NS_STEPS):
        if is_tall:
            gram_mat = jnp.einsum("bri,brj->bij", iterate, iterate, preferred_element_type=jnp.float32)
        else:
            gram_mat = jnp.einsum("bir,bjr->bij", iterate, iterate, preferred_element_type=jnp.float32)
        gram_mat = gram_mat.astype(jnp.bfloat16)
        square = jnp.einsum("bij,bjk->bik", gram_mat, gram_mat, preferred_element_type=jnp.float32)
        poly_mat = (COEF_B * gram_mat.astype(jnp.float32) + COEF_C * square).astype(jnp.bfloat16)
        if is_tall:
            update = jnp.einsum("brj,bij->bri", iterate, poly_mat, preferred_element_type=jnp.float32)
        else:
            update = jnp.einsum("bij,bjr->bir", poly_mat, iterate, preferred_element_type=jnp.float32)
        iterate = (COEF_A * iterate.astype(jnp.float32) + update).astype(jnp.bfloat16)
    return iterate


def solution(mesh):
    group_size = mesh.shape["data"]

    def kind_update(grad_full, mom_rows, master_rows):
        mat_count, num_rows, num_cols = grad_full.shape[1], grad_full.shape[2], grad_full.shape[3]
        local_rows = num_rows // group_size
        grad_rows = lax.psum_scatter(grad_full[0], "data", scatter_dimension=1, tiled=True) / group_size
        new_mom = MOMENTUM * mom_rows + grad_rows
        sq_sum = lax.psum(jnp.sum(new_mom * new_mom, axis=(1, 2), keepdims=True), "data")
        start_mat = (new_mom / (jnp.sqrt(sq_sum) + NORM_EPS)).astype(jnp.bfloat16)
        copies = max(1, group_size // mat_count)
        send_buf = jnp.broadcast_to(start_mat[:, None], (mat_count, copies, local_rows, num_cols))
        send_buf = send_buf.reshape(mat_count * copies, local_rows, num_cols)
        owned_mats = lax.all_to_all(send_buf, "data", 0, 1, tiled=True)
        ortho_mat = orthogonalize(owned_mats)
        if copies == 1:
            ortho_rows = lax.all_to_all(ortho_mat, "data", 1, 0, tiled=True)
        else:
            member = lax.axis_index("data") % copies
            block_width = num_cols // copies
            col_block = lax.dynamic_slice_in_dim(ortho_mat[0], member * block_width, block_width, axis=1)
            pieces = lax.all_to_all(col_block.reshape(group_size, local_rows, block_width), "data", 0, 0, tiled=True)
            pieces = pieces.reshape(mat_count, copies, local_rows, block_width).transpose(0, 2, 1, 3)
            ortho_rows = pieces.reshape(mat_count, local_rows, num_cols)
        step_scale = 0.2 * math.sqrt(max(num_rows, num_cols))
        new_master = master_rows - LEARN_RATE * (step_scale * ortho_rows.astype(jnp.float32) + WEIGHT_DECAY * master_rows)
        param_out = lax.all_gather(new_master.astype(jnp.bfloat16), "data", axis=1, tiled=True)
        return new_mom, new_master, param_out

    def local_step(*arrays):
        num_kinds = len(arrays) // 3
        results = [kind_update(arrays[kind_index], arrays[num_kinds + kind_index], arrays[2 * num_kinds + kind_index]) for kind_index in range(num_kinds)]
        return tuple([triple[0] for triple in results] + [triple[1] for triple in results] + [triple[2] for triple in results])

    grad_spec = P(("stage", "data"), None, None, None)
    row_spec = P("stage", "data", None)
    full_spec = P("stage", None, None)
    in_specs = (grad_spec,) * 5 + (row_spec,) * 10
    out_specs = (row_spec,) * 10 + (full_spec,) * 5
    mapped = jax.shard_map(local_step, mesh=mesh, in_specs=in_specs, out_specs=out_specs, check_vma=False)
    return mapped
```

profile of v0, /device:TPU:0, one launch (start us, length us, event | category | flops | bytes accessed | tf_op | source)
XLA Modules:
  0.0 973.2 jit_solution(40004482871401343)
XLA Ops:
  10.0 22.7 %copy.58 = f32[32,448,320]{2,0,1:T(8,128)} copy(f32[32,448,320]{1,2,0:T(8,128)} %bitcast.220) | data formatting | bytes 36700160
  32.7 24.3 %reshape.500 = f32[448,10240]{1,0:T(8,128)} reshape(f32[448,32,320]{2,1,0:T(8,128)} %bitcast.217) | data formatting | bytes 36700160
  59.6 32.1 %reduce-scatter.12.cloned.1.call-done = f32[1,640,448]{1,2,0:T(8,128)} async-done(((f32[1,2560,448]{1,2,0:T(8,128)}), f32[1,640,448]{1,2,0:T(8,128)}) %reduce-scatter.12.cloned.1.call-update) | async-done | bytes 1146896 | tf_op jit(solution)/shard_map/reduce_scatter | solution.py:42
  95.1 69.1 %reduce-scatter.10.cloned.1.call-done = f32[2,112,2560]{2,1,0:T(8,128)} async-done(((f32[2,448,2560]{2,1,0:T(8,128)}), f32[2,112,2560]{2,1,0:T(8,128)}) %reduce-scatter.10.cloned.1.call-update) | async-done | bytes 2293776 | tf_op jit(solution)/shard_map/reduce_scatter | solution.py:42
  167.6 76.9 %reduce-scatter.14.cloned.1.call-done = f32[16,80,448]{2,1,0:T(8,128)} async-done(((f32[16,320,448]{2,1,0:T(8,128)}), f32[16,80,448]{2,1,0:T(8,128)}) %reduce-scatter.14.cloned.1.call-update) | async-done | bytes 2293776 | tf_op jit(solution)/shard_map/reduce_scatter | solution.py:42
  247.6 127.5 %reduce-scatter.16.cloned.1.call-done = f32[112,10240]{1,0:T(8,128)} async-done(((f32[448,10240]{1,0:T(8,128)}), f32[112,10240]{1,0:T(8,128)}) %reduce-scatter.16.cloned.1.call-update) | async-done | bytes 4587536
  375.2 7.1 reshape.501
  382.3 6.1 copy.59
  388.4 7.4 multiply_reduce_fusion
  395.8 6.4 all-reduce
  407.8 7.8 all-to-all-done
  433.0 4.3 reduce.1
  444.6 5.8 all-to-all-done.1
  459.8 14.1 %all-to-all-done.8 = bf16[16,80,448]{2,1,0:T(8,128)(2,1)S(1)} async-done(((bf16[16,80,448]{2,1,0:T(8,128)(2,1)}), bf16[16,80,448]{2,1,0:T(8,128)(2,1)S(1)}, u32[]{:S(2)}, u32[]{:S(2)}) %all-to-all-start.8) | async-done | bytes 1146912 | tf_op jit(solution)/shard_map/all_to_all | solution.py:49
  475.4 4.7 all-to-all-start.4
  501.0 6.5 all-to-all-done.4
  514.4 5.3 fusion.6
  523.4 5.8 fusion.7
  532.9 5.3 fusion.8
  541.9 5.3 fusion.9
  550.9 5.4 fusion.55
  571.3 4.3 all-to-all-start.9
  578.3 20.7 %all-to-all-done.9 = bf16[4,320,448]{2,0,1:T(4,128)(2,1)} async-done(((bf16[4,320,448]{2,0,1:T(4,128)(2,1)}), bf16[4,320,448]{2,0,1:T(4,128)(2,1)}, u32[]{:S(2)}, u32[]{:S(2)}) %all-to-all-start.9) | async-done | bytes 1146912 | tf_op jit(solution)/shard_map/all_to_all | solution.py:52
  604.3 4.6 divide_convert_fusion
  609.0 22.9 %all-to-all-done.2 = bf16[4,112,2560]{2,1,0:T(8,128)(2,1)S(1)} async-done(((bf16[4,112,2560]{2,1,0:T(8,128)(2,1)}), bf16[4,112,2560]{2,1,0:T(8,128)(2,1)S(1)}, u32[]{:S(2)}, u32[]{:S(2)}) %all-to-all-start.2) | async-done | bytes 2293792 | tf_op jit(solution)/shard_map/all_to_all | solution.py:49
  647.3 35.2 %all-to-all-done.6 = bf16[32,112,320]{1,2,0:T(8,128)(2,1)S(1)} async-done(((bf16[32,112,320]{1,2,0:T(8,128)(2,1)}), bf16[32,112,320]{1,2,0:T(8,128)(2,1)S(1)}, u32[]{:S(2)}, u32[]{:S(2)}) %all-to-all-start.6) | async-done | bytes 2293792 | tf_op jit(solution)/shard_map/all_to_all | solution.py:49
  686.0 4.3 all_to_all.92
  690.3 5.3 fusion.2
  699.3 5.3 fusion.3
  708.4 5.3 fusion.4
  717.4 5.3 fusion.5
  726.4 5.4 fusion.56
  735.0 4.3 all-to-all-start.3
  742.6 7.1 add_convert_fusion.4
  749.6 4.9 all-to-all-done.3
  762.9 7.1 add_convert_fusion.3
  770.0 5.5 fusion.201
  775.4 7.1 add_convert_fusion.2
  782.5 5.5 fusion.202
  788.0 7.1 add_convert_fusion.1
  795.0 5.7 fusion.203
  800.7 7.1 add_convert_fusion
  811.6 35.2 %all_to_all.109 = bf16[8,448,320]{2,0,1:T(8,128)(2,1)S(1)} all-to-all(bf16[8,448,320]{2,0,1:T(8,128)(2,1)S(1)} %copy.51), channel_id=1, replica_groups=mesh['stage'=2,'data'=4] {'data'}, dimensions={1} | all-to-all | bytes 4587520 | tf_op jit(solution)/shard_map/all_to_all | solution.py:52
  849.7 6.1 copy.52
  855.8 8.0 fusion.193
  867.0 72.5 %all-gather.12.cloned.1.call-done = bf16[32,448,320]{2,0,1:T(8,128)(2,1)} async-done(((bf16[32,112,320]{2,0,1:T(8,128)(2,1)}), bf16[32,448,320]{2,0,1:T(8,128)(2,1)}) %all-gather.12.cloned.1.call-update) | async-done | bytes 9175056 | tf_op jit(solution)/shard_map/all_gather | solution.py:62
  939.5 15.7 %copy.57 = bf16[32,448,320]{1,2,0:T(8,128)(2,1)} copy(bf16[32,448,320]{2,0,1:T(8,128)(2,1)} %all-gather.12.cloned.1.call-done) | data formatting | bytes 18350080
  956.4 6.0 copy.75
  (153 shorter events, 184.5 us)
Async XLA Ops:
  7.2 49.9 %reduce-scatter.8.cloned.1.call-start = ((), (), s32[]{:S(2)}) async-start(), calls=%async_computation.15 | async-start | bytes 4587520 | tf_op jit(solution)/shard_map/reduce_scatter | solution.py:42
  7.9 83.8 %reduce-scatter.12.cloned.1.call-start = ((), (), s32[]{:S(2)}) async-start(), calls=%async_computation.17 | async-start | bytes 5734400 | tf_op jit(solution)/shard_map/reduce_scatter | solution.py:42
  8.7 155.5 %reduce-scatter.10.cloned.1.call-start = ((), (), s32[]{:S(2)}) async-start(), calls=%async_computation.16 | async-start | bytes 11468800 | tf_op jit(solution)/shard_map/reduce_scatter | solution.py:42
  9.4 235.1 %reduce-scatter.14.cloned.1.call-start = ((), (), s32[]{:S(2)}) async-start(), calls=%async_computation.18 | async-start | bytes 13107200 | tf_op jit(solution)/shard_map/reduce_scatter | solution.py:42
  10.0 365.2 %reduce-scatter.16.cloned.1.call-start = ((), (), s32[]{:S(2)}) async-start(), calls=%async_computation.24 | async-start | bytes 22937600
  57.0 1.2 copy-start.16
  59.6 343.3 %copy-start.7 = (f32[4,112,448]{2,1,0:T(8,128)}, f32[4,112,448]{2,1,0:T(8,128)S(1)}, u32[]{:S(2)}) copy-start(f32[4,112,448]{2,1,0:T(8,128)S(1)} %get-tuple-element.70) | copy-start | bytes 2408452
  59.6 104.6 %copy-start.11 = (f32[2,112,2560]{2,1,0:T(8,128)S(1)}, f32[2,112,2560]{2,1,0:T(8,128)}, u32[]{:S(2)}) copy-start(f32[2,112,2560]{2,1,0:T(8,128)} %param.21) | copy-start | bytes 6881284
  247.6 195.5 %copy-start.4 = (f32[16,80,448]{2,1,0:T(8,128)}, f32[16,80,448]{2,1,0:T(8,128)S(1)}, u32[]{:S(2)}) copy-start(f32[16,80,448]{2,1,0:T(8,128)S(1)} %get-tuple-element.74) | copy-start | bytes 6881284
  402.2 5.6 copy-start.20
  403.8 11.8 %all-to-all-start = ((bf16[4,112,448]{2,1,0:T(8,128)(2,1)}), bf16[4,112,448]{2,1,0:T(8,128)(2,1)S(1)}, u32[]{:S(2)}, u32[]{:S(2)}) async-start(bf16[4,112,448]{2,1,0:T(8,128)(2,1)} %divide_convert_fusion.4), calls=%async_computation.4 | async-start | bytes 917504 | tf_op jit(solution)/shard_map/all_to_all | solution.py:49
  439.6 10.7 %all-to-all-start.1 = ((bf16[4,2,25088]{2,1,0:T(2,128)(2,1)}), bf16[4,2,25088]{2,1,0:T(2,128)(2,1)S(1)}, u32[]{:S(2)}, u32[]{:S(2)}) async-start(bf16[4,2,25088]{2,1,0:T(2,128)(2,1)} %reshape.502), calls=%async_computation.5 | async-start | bytes 802816 | tf_op jit(solution)/shard_map/all_to_all | solution.py:52
  444.6 9.4 copy-start.19
  444.6 10.1 %copy-start.6 = (f32[1,640,448]{1,2,0:T(8,128)S(1)}, f32[1,640,448]{1,2,0:T(8,128)}, u32[]{:S(2)}) copy-start(f32[1,640,448]{1,2,0:T(8,128)} %get-tuple-element.72) | copy-start | bytes 3440644
  450.4 4.3 copy-start.14
  450.4 23.5 %all-to-all-start.8 = ((bf16[16,80,448]{2,1,0:T(8,128)(2,1)}), bf16[16,80,448]{2,1,0:T(8,128)(2,1)S(1)}, u32[]{:S(2)}, u32[]{:S(2)}) async-start(bf16[16,80,448]{2,1,0:T(8,128)(2,1)} %divide_convert_fusion.1), calls=%async_computation.12 | async-start | bytes 2621440 | tf_op jit(solution)/shard_map/all_to_all | solution.py:49
  453.9 413.0 %all-gather.6.cloned.1.call-start = ((), (), s32[]{:S(2)}) async-start(), calls=%async_computation.19 | async-start | bytes 2293760 | tf_op jit(solution)/shard_map/all_gather | solution.py:62
  457.1 1.4 copy-start.17
  475.4 32.0 %all-to-all-start.4 = ((bf16[4,640,448]{1,2,0:T(8,128)(2,1)}), bf16[4,640,448]{1,2,0:T(8,128)(2,1)}, u32[]{:S(2)}, u32[]{:S(2)}) async-start(bf16[4,640,448]{1,2,0:T(8,128)(2,1)} %reshape.497), calls=%async_computation.8 | async-start | bytes 4587520 | tf_op jit(solution)/shard_map/all_to_all | solution.py:49
  558.7 12.6 %all-to-all-start.5 = ((bf16[4,640,112]{1,2,0:T(8,128)(2,1)}), bf16[4,640,112]{1,2,0:T(8,128)(2,1)S(1)}, u32[]{:S(2)}, u32[]{:S(2)}) async-start(bf16[4,640,112]{1,2,0:T(8,128)(2,1)} %bitcast.215), calls=%async_computation.9 | async-start | bytes 1146880 | tf_op jit(solution)/shard_map/all_to_all | solution.py:57
  569.5 6.3 copy-start.15
  571.3 27.7 %all-to-all-start.9 = ((bf16[4,320,448]{2,0,1:T(4,128)(2,1)}), bf16[4,320,448]{2,0,1:T(4,128)(2,1)}, u32[]{:S(2)}, u32[]{:S(2)}) async-start(bf16[4,320,448]{2,0,1:T(4,128)(2,1)} %copy.54), calls=%async_computation.13 | async-start | bytes 2621440 | tf_op jit(solution)/shard_map/all_to_all | solution.py:52
  575.6 291.3 %all-gather.10.cloned.1.call-start = ((), (), s32[]{:S(2)}) async-start(), calls=%async_computation.21 | async-start | bytes 2867200 | tf_op jit(solution)/shard_map/all_gather | solution.py:62
  575.8 2.3 copy-start.5
  600.5 3.8 copy-start.18
  600.6 31.3 %all-to-all-start.2 = ((bf16[4,112,2560]{2,1,0:T(8,128)(2,1)}), bf16[4,112,2560]{2,1,0:T(8,128)(2,1)S(1)}, u32[]{:S(2)}, u32[]{:S(2)}) async-start(bf16[4,112,2560]{2,1,0:T(8,128)(2,1)} %bitcast.11), calls=%async_computation.6 | async-start | bytes 4587520 | tf_op jit(solution)/shard_map/all_to_all | solution.py:49
  631.8 1.4 copy-start.10
  633.2 49.2 %all-to-all-start.6 = ((bf16[32,112,320]{1,2,0:T(8,128)(2,1)}), bf16[32,112,320]{1,2,0:T(8,128)(2,1)S(1)}, u32[]{:S(2)}, u32[]{:S(2)}) async-start(bf16[32,112,320]{1,2,0:T(8,128)(2,1)} %divide_convert_fusion), calls=%async_computation.10 | async-start | bytes 5242880 | tf_op jit(solution)/shard_map/all_to_all | solution.py:49
  636.9 230.1 %all-gather.14.cloned.1.call-start = ((), (), s32[]{:S(2)}) async-start(), calls=%async_computation.23 | async-start | bytes 6553600 | tf_op jit(solution)/shard_map/all_gather | solution.py:62
  639.1 1.7 copy-start.8
  735.0 19.5 %all-to-all-start.3 = ((bf16[4,112,1280]{2,1,0:T(8,128)(2,1)}), bf16[4,112,1280]{2,1,0:T(8,128)(2,1)}, u32[]{:S(2)}, u32[]{:S(2)}) async-start(bf16[4,112,1280]{2,1,0:T(8,128)(2,1)} %bitcast.233), calls=%async_computation.7 | async-start | bytes 2293760 | tf_op jit(solution)/shard_map/all_to_all | solution.py:57
  739.3 127.7 %all-gather.8.cloned.1.call-start = ((), (), s32[]{:S(2)}) async-start(), calls=%async_computation.20 | async-start | bytes 5734400 | tf_op jit(solution)/shard_map/all_gather | solution.py:62
  756.0 1.6 copy-start.12
  757.7 2.5 copy-start
  759.9 179.6 %all-gather.12.cloned.1.call-start = ((), (), s32[]{:S(2)}) async-start(), calls=%async_computation.22 | async-start | bytes 13762560 | tf_op jit(solution)/shard_map/all_gather | solution.py:62
  770.0 5.5 copy-start.1
  782.5 5.5 copy-start.2
  795.0 5.7 copy-start.3
  866.9 88.3 %copy-start.13 = (bf16[4,448,448]{2,1,0:T(8,128)(2,1)S(1)}, bf16[4,448,448]{2,1,0:T(8,128)(2,1)}, u32[]{:S(2)}) copy-start(bf16[4,448,448]{2,1,0:T(8,128)(2,1)} %all-gather.6.cloned.1.call-done) | copy-start | bytes 4816900
  955.2 8.6 slice-start
  956.4 6.0 copy-start.9
  956.4 7.4 slice-start.1
Sparse Core Ops, SparseCore 0:
  10.5 37.8 reduce-scatter.7
  50.9 40.7 reduce-scatter.11
  94.3 69.8 reduce-scatter.9
  166.6 77.8 reduce-scatter.13
  247.0 128.1 reduce-scatter.15
  459.9 22.1 all-gather.5
  578.0 28.2 all-gather.9
  643.7 53.8 all-gather.13
  760.1 35.3 all-gather.7
  867.0 72.4 all-gather.11
where the time goes:
time: 982 us; the launch traced here: 973 us
  waiting for transfers between devices  500 us (51%)
  matrix products  189 us (19%)
  local copies, waits for them, and re-layouts  131 us (13%)
  other arithmetic  59.3 us (6%)
  blocking collectives  41.6 us (4%)
  starting transfers between devices  36 us (4%)
  between operations  15.6 us (2%)
    reduce_scatter x4, waiting for transfers between devices, kind_update(): lax.psum_scatter(grad_full[0], 'data', scatter_dimension=1, tiled=True)  178 us
    unnamed x11, waiting for transfers between devices  130 us
    unnamed x59, local copies, waits for them, and re-layouts  97.8 us
    all_to_all x5, waiting for transfers between devices, kind_update(): owned_mats = lax.all_to_all(send_buf, 'data', 0, 1, tiled=True)  86.4 us
    all_gather x5, waiting for transfers between devices, kind_update(): lax.all_gather(new_master.astype(jnp.bfloat16), 'data', axis=1, tiled=True)  72.6 us
    dot_general x10, matrix products, orthogonalize(): jnp.einsum('brj,bij->bri', iterate, poly_mat, preferred_element_type=jnp....  62.4 us
    dot_general x15, matrix products, orthogonalize(): jnp.einsum('bij,bjr->bir', poly_mat, iterate, preferred_element_type=jnp....  53.6 us
    dot_general x10, matrix products, orthogonalize(): jnp.einsum('bri,brj->bij', iterate, iterate, preferred_element_type=jnp.f...  40.7 us
  transfers between devices with their start and end apart: 19, of which 14 were waited for; matrix products, arithmetic and copies ran while one was open for 30% of the time, Pallas kernels for 0%

commit v1 on v0

v1 whole, which is shorter than its diff:
```python
import functools
import math
import jax
import jax.numpy as jnp
from jax import lax
from jax.experimental import pallas as pl
from jax.experimental.pallas import tpu as pltpu
from jax.sharding import PartitionSpec as P

NS_STEPS = 5
MOMENTUM = 0.95
LEARN_RATE = 0.2
WEIGHT_DECAY = 0.25
NORM_EPS = 1e-7
COEF_A = 3.4445
COEF_B = -4.7750
COEF_C = 2.0315
F32 = jnp.float32
BF16 = jnp.bfloat16

UNIT_MATS = (2, 2, 1, 4, 4)
ORDER = (3, 2, 1, 0, 4)
LAGS = (0, 2, 3, 4, 5, 6, 7)


class Kind:
    def __init__(self, index, count, rows, cols):
        self.index = index
        self.count, self.rows, self.cols = count, rows, cols
        self.quarter = rows // 4
        self.unit = UNIT_MATS[index]
        self.units = count // self.unit
        self.split = self.unit % 2 == 0
        self.half = self.unit // 2 if self.split else self.unit
        self.single = self.units == 1
        self.tall = rows > cols
        self.scale = 0.2 * math.sqrt(max(rows, cols))
        if index == 1:
            self.chunks = [(0, 1, 0, self.quarter), (1, 1, 0, self.quarter)]
        elif index == 2:
            step = self.quarter // 2
            self.chunks = [(0, 1, 0, step), (0, 1, step, step)]
        else:
            self.chunks = [(0, self.unit, 0, self.quarter)]

    def scratch(self):
        unit, quarter, cols = self.unit, self.quarter, self.cols
        _, cmats, _, crows = self.chunks[0]
        chunk = pltpu.VMEM((cmats, crows, cols), F32)
        shapes = dict(
            gf=chunk, df=chunk, gn=chunk, dn=chunk, xl=chunk,
            mo=pltpu.VMEM((1 if self.single else 2, unit, quarter, cols), F32),
            sb=pltpu.VMEM((1 if self.single else 2, unit, quarter, cols), F32),
            xs=pltpu.VMEM((1 if self.single else 2, unit, quarter, cols), BF16),
            pb=pltpu.VMEM((unit, quarter, cols), BF16),
            xg=pltpu.VMEM((self.units, self.half, self.rows, cols), BF16),
            nr=pltpu.VMEM((self.units, 4, 8, 128), F32),
            d2d_s=pltpu.SemaphoreType.DMA((self.units, 2)),
            d2d_r=pltpu.SemaphoreType.DMA((self.units, 2)),
            rs_s=pltpu.SemaphoreType.DMA((self.units,)),
            rs_r=pltpu.SemaphoreType.DMA((self.units,)),
            nm_s=pltpu.SemaphoreType.DMA((self.units, 3)),
            nm_r=pltpu.SemaphoreType.DMA((self.units, 3)),
            x_s=pltpu.SemaphoreType.DMA((self.units, 3)),
            x_r=pltpu.SemaphoreType.DMA((self.units, 3)),
            p_s=pltpu.SemaphoreType.DMA((self.units, 3)),
            p_r=pltpu.SemaphoreType.DMA((self.units, 3)),
            loc=pltpu.SemaphoreType.DMA((10,)),
        )
        if not self.single:
            shapes["w"] = pltpu.VMEM((unit, quarter, cols), F32)
        if self.split:
            shapes["orow"] = pltpu.VMEM((self.units, self.half, quarter, cols), BF16)
            shapes["o_s"] = pltpu.SemaphoreType.DMA((self.units,))
            shapes["o_r"] = pltpu.SemaphoreType.DMA((self.units,))
        return shapes


def dot(left, right, dims):
    return lax.dot_general(left, right, (dims, ((), ())), preferred_element_type=F32)


def newton_schulz(kind, xg, u, gram_acc):
    rows, cols = kind.rows, kind.cols

    def poly(gram_mat):
        square = dot(gram_mat, gram_mat, ((1,), (0,)))
        return (COEF_B * gram_mat.astype(F32) + COEF_C * square).astype(BF16)

    if kind.index == 2:
        block = 512

        def iteration(_, carry):
            gram_acc[...] = jnp.zeros_like(gram_acc)

            def add(b, c):
                part = xg[u, 0, pl.ds(pl.multiple_of(b * block, block), block), :]
                gram_acc[...] += dot(part, part, ((0,), (0,)))
                return c

            lax.fori_loop(0, rows // block, add, 0)
            poly_mat = poly(gram_acc[...].astype(BF16))

            def apply(b, c):
                cut = pl.ds(pl.multiple_of(b * block, block), block)
                part = xg[u, 0, cut, :]
                update = dot(part, poly_mat, ((1,), (1,)))
                xg[u, 0, cut, :] = (COEF_A * part.astype(F32) + update).astype(BF16)
                return c

            lax.fori_loop(0, rows // block, apply, 0)
            return carry
    elif kind.index == 1:
        block = 512

        def iteration(_, carry):
            gram_acc[...] = jnp.zeros_like(gram_acc)

            def add(b, c):
                part = xg[u, 0, :, pl.ds(pl.multiple_of(b * block, block), block)]
                gram_acc[...] += dot(part, part, ((1,), (1,)))
                return c

            lax.fori_loop(0, cols // block, add, 0)
            poly_mat = poly(gram_acc[...].astype(BF16))

            def apply(b, c):
                cut = pl.ds(pl.multiple_of(b * block, block), block)
                part = xg[u, 0, :, cut]
                update = dot(poly_mat, part, ((1,), (0,)))
                xg[u, 0, :, cut] = (COEF_A * part.astype(F32) + update).astype(BF16)
                return c

            lax.fori_loop(0, cols // block, apply, 0)
            return carry
    else:

        def iteration(_, carry):
            for j in range(kind.half):
                mat = xg[u, j]
                if kind.tall:
                    gram_mat = dot(mat, mat, ((0,), (0,))).astype(BF16)
                    update = dot(mat, poly(gram_mat), ((1,), (1,)))
                else:
                    gram_mat = dot(mat, mat, ((1,), (1,))).astype(BF16)
                    update = dot(poly(gram_mat), mat, ((1,), (0,)))
                xg[u, j] = (COEF_A * mat.astype(F32) + update).astype(BF16)
            return carry

    lax.fori_loop(0, NS_STEPS, iteration, 0)


def kernel(kinds, names, *refs):
    num = len(kinds)
    grads, moms, masters = refs[:num], refs[num:2 * num], refs[2 * num:3 * num]
    outs = refs[3 * num:8 * num]
    new_moms, new_masters, params, lands, far_lands = [outs[i * num:(i + 1) * num] for i in range(5)]
    rest = list(refs[8 * num:])
    bufs = []
    for k in range(num):
        bufs.append({name: rest.pop(0) for name in names[k]})
    gram_acc = rest.pop(0)

    me = lax.axis_index("data")
    chip, core = me // 2, me % 2
    far, other = 1 - chip, 1 - core
    partner, far_same, far_other = 2 * chip + other, 2 * far + core, 2 * far + other

    def to(device):
        return dict(device_id={"data": device}, device_id_type=pl.DeviceIdType.MESH)

    def remote(src, dst, send, recv, device):
        return pltpu.make_async_remote_copy(src_ref=src, dst_ref=dst, send_sem=send, recv_sem=recv, **to(device))

    def local(src, dst, sem):
        return pltpu.make_async_copy(src, dst, sem)

    barrier = pltpu.get_barrier_semaphore()
    for device in (partner, far_same, far_other):
        pl.semaphore_signal(barrier, inc=1, **to(device))
    pl.semaphore_wait(barrier, 3)

    def rows_of(kind, device, offset=0, size=None):
        size = kind.quarter if size is None else size
        return pl.ds(pl.multiple_of(device * kind.quarter + offset, 16), size)

    class Stage:
        def __init__(self, kind):
            self.kind = kind
            self.b = bufs[kind.index]
            self.grad, self.mom, self.master = grads[kind.index], moms[kind.index], masters[kind.index]
            self.new_mom, self.new_master, self.param = new_moms[kind.index], new_masters[kind.index], params[kind.index]
            self.land, self.far_land = lands[kind.index], far_lands[kind.index]

        def mats(self, u, offset=0, size=None):
            kind = self.kind
            return pl.ds(u * kind.unit + offset, kind.unit if size is None else size)

        def slot(self, u):
            return 0 if self.kind.single else u % 2

        def exchange(self, u):
            kind, b = self.kind, self.b
            mats = self.mats(u)
            return [
                remote(self.grad.at[0, mats, rows_of(kind, quarter), :], self.land.at[mats, i],
                       b["d2d_s"].at[u, i], b["d2d_r"].at[u, i], partner)
                for i, quarter in enumerate((far_other, partner))
            ]

        def load_pair(self, u, chunk, which):
            kind, b = self.kind, self.b
            mat, nmat, row, nrow = chunk
            mats = self.mats(u, mat, nmat)
            quarter, g, d, i = (far_same, "gf", "df", 0) if which == 0 else (me, "gn", "dn", 1)
            return [
                local(self.grad.at[0, mats, rows_of(kind, quarter, row, nrow), :], b[g], b["loc"].at[2 * i]),
                local(self.land.at[mats, i, pl.ds(row, nrow), :], b[d], b["loc"].at[2 * i + 1]),
            ]

        def load_mom(self, u):
            return local(self.mom.at[self.mats(u)], self.b["mo"].at[self.slot(u)], self.b["loc"].at[4])

        def weight(self):
            return self.b["sb"].at[0] if self.kind.single else self.b["w"]

        def load_weight(self, u):
            return local(self.master.at[self.mats(u)], self.weight(), self.b["loc"].at[5])

        def partial_send(self, u):
            b = self.b
            return remote(b["sb"].at[self.slot(u)], self.far_land.at[self.mats(u)], b["rs_s"].at[u], b["rs_r"].at[u], far_same)

        def first_loads(self, u):
            for i, copy in enumerate(self.exchange(u)):
                copy.wait()
            for copy in self.load_pair(u, self.kind.chunks[0], 0):
                copy.start()

        def partial(self, u):
            kind, b = self.kind, self.b
            for index, chunk in enumerate(kind.chunks):
                mat, nmat, row, nrow = chunk
                copies = self.load_pair(u, chunk, 0)
                if index:
                    for copy in copies:
                        copy.start()
                for copy in copies:
                    copy.wait()
                b["sb"][self.slot(u), mat:mat + nmat, row:row + nrow, :] = b["gf"][...] + b["df"][...]

        def partial_start(self, u):
            self.partial_send(u).start()

        def second_loads(self, u):
            for copy in self.load_pair(u, self.kind.chunks[0], 1):
                copy.start()
            self.load_mom(u).start()

        def norm_sends(self, u):
            b = self.b
            return [
                remote(b["nr"].at[u, me], b["nr"].at[u, me], b["nm_s"].at[u, i], b["nm_r"].at[u, i], device)
                for i, device in enumerate((partner, far_same, far_other))
            ]

        def mom_out(self, u):
            return local(self.b["mo"].at[self.slot(u)], self.new_mom.at[self.mats(u)], self.b["loc"].at[7])

        def momentum(self, u):
            kind, b = self.kind, self.b
            slot = self.slot(u)
            self.partial_send(u).wait()
            self.load_mom(u).wait()
            sums = [None] * kind.unit
            for index, chunk in enumerate(kind.chunks):
                mat, nmat, row, nrow = chunk
                far_copy = local(self.far_land.at[self.mats(u, mat, nmat), pl.ds(row, nrow), :], b["xl"], b["loc"].at[6])
                far_copy.start()
                copies = self.load_pair(u, chunk, 1)
                if index:
                    for copy in copies:
                        copy.start()
                for copy in copies:
                    copy.wait()
                far_copy.wait()
                for i in range(nmat):
                    total = (b["gn"][i] + b["dn"][i]) + b["xl"][i]
                    value = MOMENTUM * b["mo"][slot, mat + i, row:row + nrow, :] + total * 0.25
                    b["mo"][slot, mat + i, row:row + nrow, :] = value
                    sq_sum = jnp.sum(jnp.sum(value * value, axis=0, keepdims=True), axis=1, keepdims=True)
                    sums[mat + i] = sq_sum if sums[mat + i] is None else sums[mat + i] + sq_sum
            for i in range(kind.unit):
                b["nr"][u, me, i:i + 1, :] = jnp.broadcast_to(sums[i], (1, 128))
            self.mom_out(u).start()

        def norm_start(self, u):
            for copy in self.norm_sends(u):
                copy.start()

        def start_sends(self, u):
            kind, b = self.kind, self.b
            slot = self.slot(u)
            place = b["xg"].at[u, :, rows_of(kind, me), :]
            if kind.split:
                mine = b["xs"].at[slot, pl.ds(core * kind.half, kind.half)]
                theirs = b["xs"].at[slot, pl.ds(other * kind.half, kind.half)]
                routes = ((theirs, partner), (mine, far_same), (theirs, far_other))
            else:
                routes = ((b["xs"].at[slot], partner), (b["xs"].at[slot], far_same))
            return [remote(src, place, b["x_s"].at[u, i], b["x_r"].at[u, i], device) for i, (src, device) in enumerate(routes)]

        def start_forward(self, u):
            kind, b = self.kind, self.b
            place = b["xg"].at[u, :, rows_of(kind, far_same), :]
            return remote(place, place, b["x_s"].at[u, 2], b["x_r"].at[u, 2], partner)

        def start_matrix(self, u):
            kind, b = self.kind, self.b
            slot = self.slot(u)
            for copy in self.norm_sends(u):
                copy.wait()
            total = ((b["nr"][u, 0] + b["nr"][u, 1]) + b["nr"][u, 2]) + b["nr"][u, 3]
            norm = jnp.sqrt(total) + NORM_EPS
            for i in range(kind.unit):
                b["xs"][slot, i] = (b["mo"][slot, i] / norm[i:i + 1, 0:1]).astype(BF16)
            if kind.split:
                b["xg"][u, :, rows_of(kind, me), :] = b["xs"][slot, pl.ds(core * kind.half, kind.half)]
            else:
                b["xg"][u, :, rows_of(kind, me), :] = b["xs"][slot]
            self.mom_out(u).wait()
            for copy in self.start_sends(u):
                copy.start()

        def ortho_send(self, u):
            kind, b = self.kind, self.b
            return remote(b["xg"].at[u, :, rows_of(kind, partner), :], b["orow"].at[u], b["o_s"].at[u], b["o_r"].at[u], partner)

        def iterate(self, u):
            for copy in self.start_sends(u):
                copy.wait()
            if not self.kind.split:
                forward = self.start_forward(u)
                forward.start()
                forward.wait()
            newton_schulz(self.kind, self.b["xg"], u, gram_acc)

        def iterate_start(self, u):
            if self.kind.split:
                self.ortho_send(u).start()

        def weight_out(self, u):
            return local(self.weight(), self.new_master.at[self.mats(u)], self.b["loc"].at[8])

        def param_out(self, u):
            return local(self.b["pb"], self.param.at[self.mats(u), rows_of(self.kind, me), :], self.b["loc"].at[9])

        def param_sends(self, u):
            kind, b = self.kind, self.b
            place = self.param.at[self.mats(u), rows_of(kind, me), :]
            return [
                remote(b["pb"], place, b["p_s"].at[u, i], b["p_r"].at[u, i], device)
                for i, device in enumerate((partner, far_same))
            ]

        def param_forward(self, u):
            kind, b = self.kind, self.b
            place = self.param.at[self.mats(u), rows_of(kind, far_same), :]
            return remote(place, place, b["p_s"].at[u, 2], b["p_r"].at[u, 2], partner)

        def update(self, u):
            kind, b = self.kind, self.b
            self.load_weight(u).wait()
            weight = self.weight()
            if kind.split:
                self.ortho_send(u).wait()
                parts = ((core * kind.half, lambda j: b["xg"][u, j, rows_of(kind, me), :]),
                         (other * kind.half, lambda j: b["orow"][u, j]))
            else:
                parts = ((0, lambda j: b["xg"][u, j, rows_of(kind, me), :]),)
            for base, ortho in parts:
                for j in range(kind.half):
                    old = weight[base + j]
                    new = old - LEARN_RATE * (kind.scale * ortho(j).astype(F32) + WEIGHT_DECAY * old)
                    weight[base + j] = new
                    b["pb"][base + j] = new.astype(BF16)

        def update_start(self, u):
            self.weight_out(u).start()
            self.param_out(u).start()
            for copy in self.param_sends(u):
                copy.start()

        def forward(self, u):
            self.weight_out(u).wait()
            self.param_out(u).wait()
            for copy in self.param_sends(u):
                copy.wait()
            self.param_forward(u).start()

        def finish(self, u):
            self.param_forward(u).wait()

    stages = [Stage(kind) for kind in kinds]
    bases = {}
    total_units = 0
    for k in ORDER:
        bases[k] = total_units
        total_units += kinds[k].units

    for k in ORDER:
        stage = stages[k]

        def send_all(u, carry, stage=stage):
            for copy in stage.exchange(u):
                copy.start()
            return carry

        lax.fori_loop(0, kinds[k].units, send_all, 0)

    def step(t, carry):
        def run(name, lag):
            for k in ORDER:
                u = t - lag - bases[k]

                @pl.when((u >= 0) & (u < kinds[k].units))
                def _(k=k, u=u):
                    getattr(stages[k], name)(u)

        run("finish", LAGS[6])
        run("forward", LAGS[5])
        run("start_matrix", LAGS[2])
        run("load_weight_start", LAGS[4])
        run("first_loads", LAGS[0])
        run("second_loads", LAGS[1])
        run("iterate", LAGS[3])
        run("update", LAGS[4])
        run("iterate_start", LAGS[3])
        run("update_start", LAGS[4])
        run("momentum", LAGS[1])
        run("partial", LAGS[0])
        run("norm_start", LAGS[1])
        run("partial_start", LAGS[0])
        return carry

    Stage.load_weight_start = lambda self, u: self.load_weight(u).start()
    lax.fori_loop(0, total_units + LAGS[-1], step, 0)


def solution(mesh):
    def local_step(*arrays):
        num = len(arrays) // 3
        kinds = [Kind(k, *arrays[k].shape[1:]) for k in range(num)]
        scratch = [kind.scratch() for kind in kinds]
        names = [tuple(shapes) for shapes in scratch]
        flat = [shape for shapes in scratch for shape in shapes.values()]
        flat.append(pltpu.VMEM((kinds[1].rows, kinds[1].rows), F32))
        row_shapes = [jax.ShapeDtypeStruct((kind.count, kind.quarter, kind.cols), F32) for kind in kinds]
        full_shapes = [jax.ShapeDtypeStruct((kind.count, kind.rows, kind.cols), BF16) for kind in kinds]
        land_shapes = [jax.ShapeDtypeStruct((kind.count, 2, kind.quarter, kind.cols), F32) for kind in kinds]
        outs = pl.pallas_call(
            functools.partial(kernel, kinds, names),
            out_shape=row_shapes + row_shapes + full_shapes + land_shapes + row_shapes,
            in_specs=[pl.BlockSpec(memory_space=pl.ANY)] * (3 * num),
            out_specs=[pl.BlockSpec(memory_space=pl.ANY)] * (5 * num),
            scratch_shapes=flat,
            compiler_params=pltpu.CompilerParams(
                collective_id=0, has_side_effects=True, vmem_limit_bytes=67043328
            ),
        )(*arrays)
        return tuple(outs[:3 * num])

    grad_spec = P(("stage", "data"), None, None, None)
    row_spec = P("stage", "data", None)
    full_spec = P("stage", None, None)
    in_specs = (grad_spec,) * 5 + (row_spec,) * 10
    out_specs = (row_spec,) * 10 + (full_spec,) * 5
    return jax.shard_map(local_step, mesh=mesh, in_specs=in_specs, out_specs=out_specs, check_vma=False)
```

time: 982 us -> 687 us (0.70)
  Pallas kernels: 0 us -> 586 us
  waiting for transfers between devices: 500 us -> 0 us
  matrix products: 189 us -> 0 us
  other arithmetic: 59.3 us -> 0.01 us
  blocking collectives: 41.6 us -> 0 us
  starting transfers between devices: 36 us -> 0 us
  local copies, waits for them, and re-layouts: 131 us -> 97.8 us
  between operations: 15.6 us -> 0.7 us
    pallas_call x0 -> x1, Pallas kernels: none -> 586 us  [local_step(): pl.pallas_call(functools.partial(kernel, kinds, names), out_shape=row_sha...]
    dot_general x50 -> x0, matrix products: 189 us -> none  [the longest x10 62.4 us: orthogonalize(): jnp.einsum('brj,bij->bri', iterate, poly_mat, preferred_element_type=jnp....]
    reduce_scatter x4 -> x0, waiting for transfers between devices: 178 us -> none  [kind_update(): lax.psum_scatter(grad_full[0], 'data', scatter_dimension=1, tiled=True)]
    unnamed x11 -> x0, waiting for transfers between devices: 130 us -> none
    all_to_all x9 -> x0, waiting for transfers between devices: 120 us -> none  [the longest x5 86.4 us: kind_update(): owned_mats = lax.all_to_all(send_buf, 'data', 0, 1, tiled=True)]
    all_gather x5 -> x0, waiting for transfers between devices: 72.6 us -> none  [kind_update(): lax.all_gather(new_master.astype(jnp.bfloat16), 'data', axis=1, tiled=True)]
    all_to_all x1 -> x0, blocking collectives: 35.2 us -> none  [kind_update(): ortho_rows = lax.all_to_all(ortho_mat, 'data', 1, 0, tiled=True)]
    all_to_all x9 -> x0, starting transfers between devices: 35 us -> none  [the longest x5 19.5 us: kind_update(): owned_mats = lax.all_to_all(send_buf, 'data', 0, 1, tiled=True)]
  transfers between devices with their start and end apart: 19 -> 0, of which waited for: 14 -> 0; matrix products, arithmetic and copies ran while one was open for 30% -> 0% of each run, Pallas kernels for 0% -> 0%
where the time goes in v1:
time: 687 us; the launch traced here: 684 us
  Pallas kernels  586 us (85%)
  local copies, waits for them, and re-layouts  97.8 us (14%)
    pallas_call x1, Pallas kernels, local_step(): pl.pallas_call(functools.partial(kernel, kinds, names), out_shape=row_sha...  586 us
    unnamed x47, local copies, waits for them, and re-layouts  97.8 us

profile of v1, /device:TPU:0, one launch (start us, length us, event | category | flops | bytes accessed | tf_op | source)
XLA Modules:
  0.0 684.2 jit_solution(11039094611193389679)
XLA Ops:
  0.6 0.0 copy-start.6
  0.7 2.8 copy.32.refs_7_
  3.5 0.0 copy-done.6
  3.5 1.5 copy.34.refs_12_
  4.9 5.7 copy.30.refs_2_
  10.7 6.1 copy.33.refs_8_
  16.7 6.1 copy.35.refs_13_
  22.8 22.4 %copy.31.refs_3_ = f32[1,32,448,320]{3,2,1,0:T(8,128)} copy(f32[1,32,448,320]{2,3,1,0:T(8,128)} %param.18) | data formatting | bytes 36700160 | tf_op args[3]
  45.2 585.7 %shard_map.262 = (f32[4,112,448]{2,1,0:T(8,128)}, f32[2,112,2560]{2,1,0:T(8,128)}, f32[1,640,448]{2,1,0:T(8,128)}, f32[32,112,320]{2,1,0:T(8,128)}, f32[16,80,44...) custom-call(f32[1,4,448,448]{3,2,1,0:T(8,128)} %refs_0_.1, ...), custom_call_target="tpu_custom_call" | custom-call | tf_op jit(solution)/shard_map/pallas_call | solution.py:461
  630.9 0.0 copy-start.2
  630.9 2.9 copy.36
  633.8 2.7 copy.38
  636.5 0.0 copy-done.2
  636.5 2.5 copy.40
  639.0 6.1 copy.37
  645.1 6.1 copy.39
  651.2 0.0 copy-start.8
  651.2 0.0 copy-start.4
  651.2 14.7 %copy.41 = bf16[32,448,320]{1,2,0:T(8,128)(2,1)} copy(bf16[32,448,320]{2,1,0:T(8,128)(2,1)} %get-tuple-element.58) | data formatting | bytes 18350080
  665.9 0.0 copy-done.8
  665.9 0.9 copy.51
  666.8 0.0 copy-done.4
  666.8 0.0 copy-start.1
  666.8 1.4 copy.52
  668.2 1.2 copy-done.1
  669.4 0.0 copy-start.7
  669.4 0.0 copy-start.3
  669.4 1.5 copy.53
  670.9 0.3 copy-done.7
  671.2 0.0 copy-start
  671.2 0.9 copy.54
  672.1 0.3 copy-done.3
  672.5 0.0 slice-start.2
  672.5 1.4 copy.55
  673.8 0.0 copy-done
  673.8 0.0 copy-start.5
  673.9 0.0 slice-start.3
  673.9 1.5 copy.56
  675.3 1.6 copy-done.5
  676.9 0.0 slice-start
  676.9 1.2 copy.57
  678.2 0.0 slice-done.2
  678.2 0.0 slice-done.3
  678.2 0.0 slice-start.1
  678.2 2.3 copy.58
  680.5 1.0 slice-done
  681.5 0.4 slice-done.1
  681.9 2.4 copy.59
  (2 shorter events, 0.0 us)
Async XLA Ops:
  0.6 2.8 copy-start.6
  630.9 5.6 copy-start.2
  651.2 14.7 %copy-start.8 = (f32[4,112,448]{2,1,0:T(8,128)S(1)}, f32[4,112,448]{2,1,0:T(8,128)}, u32[]{:S(2)}) copy-start(f32[4,112,448]{2,1,0:T(8,128)} %get-tuple-element.75) | copy-start | bytes 2408452
  651.2 15.6 %copy-start.4 = (f32[2,112,2560]{2,1,0:T(8,128)S(1)}, f32[2,112,2560]{2,1,0:T(8,128)}, u32[]{:S(2)}) copy-start(f32[2,112,2560]{2,1,0:T(8,128)} %get-tuple-element.76) | copy-start | bytes 6881284
  666.8 2.6 copy-start.1
  669.4 1.8 copy-start.7
  669.4 3.1 copy-start.3
  671.2 2.6 copy-start
  672.5 5.7 slice-start.2
  673.8 3.1 copy-start.5
  673.9 4.3 slice-start.3
  676.9 4.5 slice-start
  678.2 3.7 slice-start.1

commit v2 on v1

v2 whole, which is shorter than its diff:
```python
import functools
import math
import jax
import jax.numpy as jnp
from jax import lax
from jax.experimental import pallas as pl
from jax.experimental.pallas import tpu as pltpu
from jax.sharding import PartitionSpec as P

NS_STEPS = 5
MOMENTUM = 0.95
LEARN_RATE = 0.2
WEIGHT_DECAY = 0.25
NORM_EPS = 1e-7
COEF_A = 3.4445
COEF_B = -4.7750
COEF_C = 2.0315
F32 = jnp.float32
BF16 = jnp.bfloat16

UNIT_MATS = (2, 2, 1, 4, 4)
ORDER = (3, 2, 1, 0, 4)
LAGS = (0, 2, 3, 4, 5, 6, 7, 8)
SCHEDULE = (
    ("close", 7), ("finish", 6), ("forward", 5), ("combine", 1), ("start_matrix", 2),
    ("load_weight_start", 4), ("first_loads", 0), ("second_loads", 1),
    ("start_start", 2), ("combine_start", 1),
    ("iterate", 3), ("update", 4), ("iterate_start", 3), ("update_start", 4),
    ("momentum", 1), ("partial", 0), ("norm_start", 1), ("partial_start", 0),
)


class Kind:
    def __init__(self, index, count, rows, cols):
        self.index = index
        self.scale = 0.2 * math.sqrt(max(rows, cols))
        self.flip = index in (2, 3)
        if self.flip:
            rows, cols = cols, rows
        self.lanes = index == 3
        self.count, self.rows, self.cols = count, rows, cols
        self.q_rows, self.q_cols = (rows, cols // 4) if self.flip else (rows // 4, cols)
        self.unit = UNIT_MATS[index]
        self.units = count // self.unit
        self.split = self.unit % 2 == 0
        self.half = self.unit // 2 if self.split else self.unit
        self.single = self.units == 1
        if index == 1:
            self.chunks = [(0, 1, 0, self.q_rows), (1, 1, 0, self.q_rows)]
        elif index == 2:
            step = self.q_rows // 2
            self.chunks = [(0, 1, 0, step), (0, 1, step, step)]
        else:
            self.chunks = [(0, self.unit, 0, self.q_rows)]

    def sems(self):
        shapes = {name: pltpu.SemaphoreType.DMA((self.units, 3)) for name in (
            "d2d_s", "d2d_r", "rs_s", "rs_r", "nm_s", "nm_r", "x_s", "x_r", "o_s", "o_r", "p_s", "p_r", "t_s", "t_r")}
        shapes["loc"] = pltpu.SemaphoreType.DMA((10,))
        return shapes

    def scratch(self):
        if self.lanes:
            return self.lane_scratch()
        unit, q_rows, q_cols = self.unit, self.q_rows, self.q_cols
        slots = 1 if self.single else 2
        _, cmats, _, crows = self.chunks[0]
        chunk = pltpu.VMEM((cmats, crows, q_cols), F32)
        shapes = dict(
            gf=chunk, df=chunk, xl=chunk,
            mo=pltpu.VMEM((slots, unit, q_rows, q_cols), F32),
            sb=pltpu.VMEM((slots, unit, q_rows, q_cols), F32),
            xs=pltpu.VMEM((slots, unit, q_rows, q_cols), BF16),
            xg=pltpu.VMEM((self.units, self.half, self.rows, self.cols), BF16),
            nr=pltpu.VMEM((self.units, 4, 8, 128), F32),
        )
        if not self.single:
            shapes["gn"] = chunk
            shapes["dn"] = chunk
            shapes["w"] = pltpu.VMEM((unit, q_rows, q_cols), F32)
            shapes["pb"] = pltpu.VMEM((unit, q_rows, q_cols), BF16)
        if self.split:
            shapes["orow"] = pltpu.VMEM((self.units, self.half, q_rows, q_cols), BF16)
        shapes.update(self.sems())
        return shapes

    def lane_scratch(self):
        unit, half, rows, cols, lanes, units = self.unit, self.half, self.rows, self.cols, self.q_cols, self.units
        shapes = dict(
            gf=pltpu.VMEM((half, rows, cols), F32),
            df=pltpu.VMEM((half, rows, cols), F32),
            sb=pltpu.VMEM((2, 7, rows // 2, 128), F32),
            nb=pltpu.VMEM((2, 2, half, rows, lanes), F32),
            xl=pltpu.VMEM((7, rows // 2, 128), F32),
            tq=pltpu.VMEM((half, rows, lanes), F32),
            tr=pltpu.VMEM((units, half, rows, lanes), F32),
            mo=pltpu.VMEM((2, unit, rows, lanes), F32),
            w=pltpu.VMEM((unit, rows, lanes), F32),
            xs=pltpu.VMEM((2, unit, rows, 128), BF16),
            xp=pltpu.VMEM((2, 2, 7, rows // 4, 128), BF16),
            xq=pltpu.VMEM((units, 2, 7, rows // 4, 128), BF16),
            xg=pltpu.VMEM((units, half, rows, 512), BF16),
            orow=pltpu.VMEM((units, half, rows, 128), BF16),
            pb=pltpu.VMEM((unit, rows, lanes), BF16),
            pk=pltpu.VMEM((7, rows // 2, 128), BF16),
            pv=pltpu.VMEM((4, 7, rows // 2, 128), BF16),
            pa=pltpu.VMEM((unit, rows, cols), BF16),
            nr=pltpu.VMEM((units, 4, 8, 128), F32),
        )
        shapes.update(self.sems())
        return shapes


def pack(pieces):
    last = pieces[7]
    return [jnp.concatenate([pieces[g], last[:, 16 * g:16 * g + 16]], axis=1) for g in range(7)]


def unpack(blocks):
    return [block[:, :112] for block in blocks] + [jnp.concatenate([block[:, 112:128] for block in blocks], axis=1)]


def dot(left, right, dims):
    return lax.dot_general(left, right, (dims, ((), ())), preferred_element_type=F32)


def newton_schulz(kind, xg, u, gram_acc):
    cols = kind.cols

    def poly(gram_mat):
        square = dot(gram_mat, gram_mat, ((1,), (0,)))
        return (COEF_B * gram_mat.astype(F32) + COEF_C * square).astype(BF16)

    if kind.single:
        block = 512

        def iteration(_, carry):
            gram_acc[...] = jnp.zeros_like(gram_acc)

            def add(b, c):
                part = xg[u, 0, :, pl.ds(pl.multiple_of(b * block, block), block)]
                gram_acc[...] += dot(part, part, ((1,), (1,)))
                return c

            lax.fori_loop(0, cols // block, add, 0)
            poly_mat = poly(gram_acc[...].astype(BF16))

            def apply(b, c):
                cut = pl.ds(pl.multiple_of(b * block, block), block)
                part = xg[u, 0, :, cut]
                update = dot(poly_mat, part, ((1,), (0,)))
                xg[u, 0, :, cut] = (COEF_A * part.astype(F32) + update).astype(BF16)
                return c

            lax.fori_loop(0, cols // block, apply, 0)
            return carry
    else:

        def iteration(_, carry):
            for j in range(kind.half):
                mat = xg[u, j]
                gram_mat = dot(mat, mat, ((1,), (1,))).astype(BF16)
                update = dot(poly(gram_mat), mat, ((1,), (0,)))
                xg[u, j] = (COEF_A * mat.astype(F32) + update).astype(BF16)
            return carry

    lax.fori_loop(0, NS_STEPS, iteration, 0)


def kernel(kinds, names, *refs):
    num = len(kinds)
    grads, moms, masters = refs[:num], refs[num:2 * num], refs[2 * num:3 * num]
    outs = refs[3 * num:8 * num]
    new_moms, new_masters, params, lands, far_lands = [outs[i * num:(i + 1) * num] for i in range(5)]
    param_land = refs[8 * num]
    rest = list(refs[8 * num + 1:])
    bufs = []
    for k in range(num):
        bufs.append({name: rest.pop(0) for name in names[k]})
    gram_acc = rest.pop(0)

    me = lax.axis_index("data")
    chip, core = me // 2, me % 2
    far, other = 1 - chip, 1 - core
    partner, far_same, far_other = 2 * chip + other, 2 * far + core, 2 * far + other

    def to(device):
        return dict(device_id={"data": device}, device_id_type=pl.DeviceIdType.MESH)

    def remote(src, dst, send, recv, device):
        return pltpu.make_async_remote_copy(src_ref=src, dst_ref=dst, send_sem=send, recv_sem=recv, **to(device))

    def local(src, dst, sem):
        return pltpu.make_async_copy(src, dst, sem)

    barrier = pltpu.get_barrier_semaphore()
    for device in (partner, far_same, far_other):
        pl.semaphore_signal(barrier, inc=1, **to(device))
    pl.semaphore_wait(barrier, 3)

    def block_of(kind, device, row=0, nrow=None):
        nrow = kind.q_rows if nrow is None else nrow
        if kind.flip:
            return pl.ds(row, nrow), pl.ds(pl.multiple_of(device * kind.q_cols, 128), kind.q_cols)
        return pl.ds(pl.multiple_of(device * kind.q_rows + row, 16), nrow), slice(None)

    class Stage:
        def __init__(self, kind):
            self.kind = kind
            self.b = bufs[kind.index]
            self.grad, self.mom, self.master = grads[kind.index], moms[kind.index], masters[kind.index]
            self.new_mom, self.new_master, self.param = new_moms[kind.index], new_masters[kind.index], params[kind.index]
            self.land, self.far_land = lands[kind.index], far_lands[kind.index]
            self.param_land = param_land

        def mats(self, u, offset=0, size=None):
            kind = self.kind
            return pl.ds(u * kind.unit + offset, kind.unit if size is None else size)

        def slot(self, u):
            return 0 if self.kind.single else u % 2

        def exchange(self, u):
            kind, b = self.kind, self.b
            mats = self.mats(u)
            return [
                remote(self.grad.at[(0, mats) + block_of(kind, quarter)], self.land.at[mats, i],
                       b["d2d_s"].at[u, i], b["d2d_r"].at[u, i], partner)
                for i, quarter in enumerate((far_other, partner))
            ]

        def load_pair(self, u, chunk, which):
            kind, b = self.kind, self.b
            mat, nmat, row, nrow = chunk
            mats = self.mats(u, mat, nmat)
            quarter, g, d, i = (far_same, "gf", "df", 0) if which == 0 else (me,) + (("gf", "df") if kind.single else ("gn", "dn")) + (1,)
            return [
                local(self.grad.at[(0, mats) + block_of(kind, quarter, row, nrow)], b[g], b["loc"].at[2 * i]),
                local(self.land.at[mats, i, pl.ds(row, nrow), :], b[d], b["loc"].at[2 * i + 1]),
            ]

        def load_mom(self, u):
            return local(self.mom.at[self.mats(u)], self.b["mo"].at[self.slot(u)], self.b["loc"].at[4])

        def weight(self):
            return self.b["sb"].at[0] if self.kind.single else self.b["w"]

        def rounded(self):
            return self.b["xs"].at[0] if self.kind.single else self.b["pb"]

        def load_weight(self, u):
            return local(self.master.at[self.mats(u)], self.weight(), self.b["loc"].at[5])

        def partial_send(self, u):
            b = self.b
            return remote(b["sb"].at[self.slot(u)], self.far_land.at[self.mats(u)], b["rs_s"].at[u, 0], b["rs_r"].at[u, 0], far_same)

        def first_loads(self, u):
            for i, copy in enumerate(self.exchange(u)):
                copy.wait()
            for copy in self.load_pair(u, self.kind.chunks[0], 0):
                copy.start()

        def partial(self, u):
            kind, b = self.kind, self.b
            for index, chunk in enumerate(kind.chunks):
                mat, nmat, row, nrow = chunk
                copies = self.load_pair(u, chunk, 0)
                if index:
                    for copy in copies:
                        copy.start()
                for copy in copies:
                    copy.wait()
                b["sb"][self.slot(u), mat:mat + nmat, row:row + nrow, :] = b["gf"][...] + b["df"][...]

        def partial_start(self, u):
            self.partial_send(u).start()

        def second_loads(self, u):
            for copy in self.load_pair(u, self.kind.chunks[0], 1):
                copy.start()
            self.load_mom(u).start()

        def norm_sends(self, u):
            b = self.b
            return [
                remote(b["nr"].at[u, me], b["nr"].at[u, me], b["nm_s"].at[u, i], b["nm_r"].at[u, i], device)
                for i, device in enumerate((partner, far_same, far_other))
            ]

        def mom_out(self, u):
            return local(self.b["mo"].at[self.slot(u)], self.new_mom.at[self.mats(u)], self.b["loc"].at[7])

        def momentum(self, u):
            kind, b = self.kind, self.b
            slot = self.slot(u)
            self.partial_send(u).wait()
            self.load_mom(u).wait()
            near_g, near_d = ("gf", "df") if kind.single else ("gn", "dn")
            sums = [None] * kind.unit
            for index, chunk in enumerate(kind.chunks):
                mat, nmat, row, nrow = chunk
                far_copy = local(self.far_land.at[self.mats(u, mat, nmat), pl.ds(row, nrow), :], b["xl"], b["loc"].at[6])
                far_copy.start()
                copies = self.load_pair(u, chunk, 1)
                if index:
                    for copy in copies:
                        copy.start()
                for copy in copies:
                    copy.wait()
                far_copy.wait()
                for i in range(nmat):
                    total = (b[near_g][i] + b[near_d][i]) + b["xl"][i]
                    value = MOMENTUM * b["mo"][slot, mat + i, row:row + nrow, :] + total * 0.25
                    b["mo"][slot, mat + i, row:row + nrow, :] = value
                    sq_sum = jnp.sum(jnp.sum(value * value, axis=0, keepdims=True), axis=1, keepdims=True)
                    sums[mat + i] = sq_sum if sums[mat + i] is None else sums[mat + i] + sq_sum
            for i in range(kind.unit):
                b["nr"][u, me, i:i + 1, :] = jnp.broadcast_to(sums[i], (1, 128))
            self.mom_out(u).start()

        def norm_start(self, u):
            for copy in self.norm_sends(u):
                copy.start()

        def start_sends(self, u):
            kind, b = self.kind, self.b
            slot = self.slot(u)
            place = b["xg"].at[(u, slice(None)) + block_of(kind, me)]
            if kind.split:
                mine = b["xs"].at[slot, pl.ds(core * kind.half, kind.half)]
                theirs = b["xs"].at[slot, pl.ds(other * kind.half, kind.half)]
                routes = ((theirs, partner), (mine, far_same), (theirs, far_other))
            else:
                routes = ((b["xs"].at[slot], partner), (b["xs"].at[slot], far_same))
            return [remote(src, place, b["x_s"].at[u, i], b["x_r"].at[u, i], device) for i, (src, device) in enumerate(routes)]

        def start_forward(self, u):
            kind, b = self.kind, self.b
            place = b["xg"].at[(u, slice(None)) + block_of(kind, far_same)]
            return remote(place, place, b["x_s"].at[u, 2], b["x_r"].at[u, 2], partner)

        def start_matrix(self, u):
            kind, b = self.kind, self.b
            slot = self.slot(u)
            for copy in self.norm_sends(u):
                copy.wait()
            total = ((b["nr"][u, 0] + b["nr"][u, 1]) + b["nr"][u, 2]) + b["nr"][u, 3]
            norm = jnp.sqrt(total) + NORM_EPS
            for i in range(kind.unit):
                b["xs"][slot, i] = (b["mo"][slot, i] / norm[i:i + 1, 0:1]).astype(BF16)
            if kind.split:
                b["xg"][(u, slice(None)) + block_of(kind, me)] = b["xs"][slot, pl.ds(core * kind.half, kind.half)]
            else:
                b["xg"][(u, slice(None)) + block_of(kind, me)] = b["xs"][slot]
            self.mom_out(u).wait()

        def start_start(self, u):
            for copy in self.start_sends(u):
                copy.start()

        def ortho_send(self, u):
            kind, b = self.kind, self.b
            return remote(b["xg"].at[(u, slice(None)) + block_of(kind, partner)], b["orow"].at[u], b["o_s"].at[u, 0], b["o_r"].at[u, 0], partner)

        def iterate(self, u):
            for copy in self.start_sends(u):
                copy.wait()
            if not self.kind.split:
                forward = self.start_forward(u)
                forward.start()
                forward.wait()
            newton_schulz(self.kind, self.b["xg"], u, gram_acc)

        def iterate_start(self, u):
            if self.kind.split:
                self.ortho_send(u).start()

        def weight_out(self, u):
            return local(self.weight(), self.new_master.at[self.mats(u)], self.b["loc"].at[8])

        def param_out(self, u):
            return local(self.rounded(), self.param.at[(self.mats(u),) + block_of(self.kind, me)], self.b["loc"].at[9])

        def param_sends(self, u):
            kind, b = self.kind, self.b
            place = self.param.at[(self.mats(u),) + block_of(kind, me)]
            return [
                remote(self.rounded(), place, b["p_s"].at[u, i], b["p_r"].at[u, i], device)
                for i, device in enumerate((partner, far_same))
            ]

        def param_forward(self, u):
            kind, b = self.kind, self.b
            place = self.param.at[(self.mats(u),) + block_of(kind, far_same)]
            return remote(place, place, b["p_s"].at[u, 2], b["p_r"].at[u, 2], partner)

        def update(self, u):
            kind, b = self.kind, self.b
            self.load_weight(u).wait()
            weight = self.weight()
            if kind.split:
                self.ortho_send(u).wait()
                parts = ((core * kind.half, lambda j: b["xg"][(u, j) + block_of(kind, me)]),
                         (other * kind.half, lambda j: b["orow"][u, j]))
            else:
                parts = ((0, lambda j: b["xg"][(u, j) + block_of(kind, me)]),)
            for base, ortho in parts:
                for j in range(kind.half):
                    old = weight[base + j]
                    new = old - LEARN_RATE * (kind.scale * ortho(j).astype(F32) + WEIGHT_DECAY * old)
                    weight[base + j] = new
                    self.rounded()[base + j] = new.astype(BF16)

        def update_start(self, u):
            self.weight_out(u).start()
            self.param_out(u).start()
            for copy in self.param_sends(u):
                copy.start()

        def forward(self, u):
            self.weight_out(u).wait()
            self.param_out(u).wait()
            for copy in self.param_sends(u):
                copy.wait()
            self.param_forward(u).start()

        def finish(self, u):
            self.param_forward(u).wait()

        def load_weight_start(self, u):
            self.load_weight(u).start()

    class LaneStage(Stage):
        def exchange(self, u):
            b = self.b
            half = self.kind.half
            src = self.grad.at[0, pl.ds(u * self.kind.unit + other * half, half)]
            return [remote(src, self.land.at[pl.ds(u * half, half)], b["d2d_s"].at[u, 0], b["d2d_r"].at[u, 0], partner)]

        def own_loads(self, u):
            b = self.b
            half = self.kind.half
            return [local(self.grad.at[0, pl.ds(u * self.kind.unit + core * half, half)], b["gf"], b["loc"].at[0]),
                    local(self.land.at[pl.ds(u * half, half)], b["df"], b["loc"].at[1])]

        def first_loads(self, u):
            for copy in self.exchange(u):
                copy.wait()
            for copy in self.own_loads(u):
                copy.start()

        def partial(self, u):
            kind, b = self.kind, self.b
            slot = self.slot(u)
            for copy in self.own_loads(u):
                copy.wait()
            cut = kind.rows // 2

            def far_piece(i, j, r):
                both = b["gf"][i, r * cut:(r + 1) * cut, :] + b["df"][i, r * cut:(r + 1) * cut, :]
                quarters = [both[:, 112 * d:112 * (d + 1)] for d in range(4)]
                if j == 0:
                    near = [jnp.where(chip == 0, quarters[d], quarters[2 + d]) for d in range(2)]
                    b["nb"][slot, 0, i, r * cut:(r + 1) * cut, :] = jnp.where(core == 0, near[0], near[1])
                    b["nb"][slot, 1, i, r * cut:(r + 1) * cut, :] = jnp.where(core == 0, near[1], near[0])
                return jnp.where(chip == 0, quarters[2 + j], quarters[j])

            last = far_piece(1, 1, 1)
            for g in range(7):
                piece = far_piece(g // 4, g // 2 % 2, g % 2)
                b["sb"][slot, g] = jnp.concatenate([piece, last[:, 16 * g:16 * g + 16]], axis=1)

        def partial_send(self, u):
            b = self.b
            return remote(b["sb"].at[self.slot(u)], self.far_land.at[u], b["rs_s"].at[u, 0], b["rs_r"].at[u, 0], far_same)

        def second_loads(self, u):
            self.load_mom(u).start()

        def combine(self, u):
            kind, b = self.kind, self.b
            slot = self.slot(u)
            self.partial_send(u).wait()
            copy = local(self.far_land.at[u], b["xl"], b["loc"].at[6])
            copy.start()
            copy.wait()
            cut = kind.rows // 2
            for i in range(kind.half):
                for r in range(2):
                    rows = slice(r * cut, (r + 1) * cut)
                    first = b["xl"][i * 4 + r][:, :112]
                    if i * 4 + 2 + r < 7:
                        second = b["xl"][i * 4 + 2 + r][:, :112]
                    else:
                        second = jnp.concatenate([b["xl"][g][:, 112:128] for g in range(7)], axis=1)
                    b["nb"][slot, 0, i, rows, :] = b["nb"][slot, 0, i, rows, :] + jnp.where(core == 0, first, second)
                    b["tq"][i, rows, :] = b["nb"][slot, 1, i, rows, :] + jnp.where(core == 0, second, first)

        def total_send(self, u):
            b = self.b
            return remote(b["tq"], b["tr"].at[u], b["t_s"].at[u, 0], b["t_r"].at[u, 0], partner)

        def combine_start(self, u):
            self.total_send(u).start()

        def momentum(self, u):
            kind, b = self.kind, self.b
            slot = self.slot(u)
            self.load_mom(u).wait()
            self.total_send(u).wait()
            for base, total in ((core * kind.half, lambda i: b["nb"][slot, 0, i]), (other * kind.half, lambda i: b["tr"][u, i])):
                for i in range(kind.half):
                    value = MOMENTUM * b["mo"][slot, base + i] + total(i) * 0.25
                    b["mo"][slot, base + i] = value
                    sq_sum = jnp.sum(jnp.sum(value * value, axis=0, keepdims=True), axis=1, keepdims=True)
                    b["nr"][u, me, pl.ds(base + i, 1), :] = jnp.broadcast_to(sq_sum, (1, 128))
            self.mom_out(u).start()

        def lane_block(self, device):
            return pl.ds(pl.multiple_of(device * 128, 128), 128)

        def start_sends(self, u):
            kind, b = self.kind, self.b
            slot = self.slot(u)
            routes = (
                (b["xs"].at[slot, pl.ds(other * kind.half, kind.half)], b["xg"].at[u, :, :, self.lane_block(me)], partner),
                (b["xp"].at[slot, 0], b["xq"].at[u, 0], far_same),
                (b["xp"].at[slot, 1], b["xq"].at[u, 1], far_other),
            )
            return [remote(src, dst, b["x_s"].at[u, i], b["x_r"].at[u, i], device) for i, (src, dst, device) in enumerate(routes)]

        def start_matrix(self, u):
            kind, b = self.kind, self.b
            slot = self.slot(u)
            for copy in self.norm_sends(u):
                copy.wait()
            total = ((b["nr"][u, 0] + b["nr"][u, 1]) + b["nr"][u, 2]) + b["nr"][u, 3]
            norm = jnp.sqrt(total) + NORM_EPS
            pad = jnp.zeros((kind.rows, 16), F32)
            for i in range(kind.unit):
                start = b["mo"][slot, i] / norm[i:i + 1, 0:1]
                b["xs"][slot, i] = jnp.concatenate([start, pad], axis=1).astype(BF16)
            b["xg"][u, :, :, self.lane_block(me)] = b["xs"][slot, pl.ds(core * kind.half, kind.half)]
            cut = kind.rows // 4
            for h, base in enumerate((core * kind.half, other * kind.half)):
                pieces = [b["xs"][slot, base + g // 4, g % 4 * cut:(g % 4 + 1) * cut, :].astype(F32)[:, :112] for g in range(8)]
                for g, block in enumerate(pack(pieces)):
                    b["xp"][slot, h, g] = block.astype(BF16)
            self.mom_out(u).wait()

        def iterate(self, u):
            kind, b = self.kind, self.b
            for copy in self.start_sends(u):
                copy.wait()
            cut = kind.rows // 4
            pad = jnp.zeros((cut, 16), F32)
            for h, device in enumerate((far_same, far_other)):
                pieces = unpack([b["xq"][u, h, g].astype(F32) for g in range(7)])
                for g, piece in enumerate(pieces):
                    block = jnp.concatenate([piece, pad], axis=1).astype(BF16)
                    b["xg"][u, g // 4, g % 4 * cut:(g % 4 + 1) * cut, self.lane_block(device)] = block
            newton_schulz(kind, b["xg"], u, gram_acc)

        def ortho_send(self, u):
            b = self.b
            return remote(b["xg"].at[u, :, :, self.lane_block(partner)], b["orow"].at[u], b["o_s"].at[u, 0], b["o_r"].at[u, 0], partner)

        def param_out(self, u):
            return local(self.b["pk"], self.param_land.at[u, me], self.b["loc"].at[9])

        def param_sends(self, u):
            b = self.b
            place = self.param_land.at[u, me]
            return [
                remote(b["pk"], place, b["p_s"].at[u, i], b["p_r"].at[u, i], device)
                for i, device in enumerate((partner, far_same))
            ]

        def param_forward(self, u):
            b = self.b
            place = self.param_land.at[u, far_same]
            return remote(place, place, b["p_s"].at[u, 2], b["p_r"].at[u, 2], partner)

        def update(self, u):
            kind, b = self.kind, self.b
            self.load_weight(u).wait()
            self.ortho_send(u).wait()
            weight = b["w"]
            parts = ((core * kind.half, lambda j: b["xg"][u, j, :, self.lane_block(me)]),
                     (other * kind.half, lambda j: b["orow"][u, j]))
            for base, ortho in parts:
                for j in range(kind.half):
                    old = weight[base + j]
                    new = old - LEARN_RATE * (kind.scale * ortho(j).astype(F32)[:, :112] + WEIGHT_DECAY * old)
                    weight[base + j] = new
                    b["pb"][base + j] = new.astype(BF16)
            cut = kind.rows // 2
            pieces = [b["pb"][g // 2, g % 2 * cut:(g % 2 + 1) * cut, :].astype(F32) for g in range(8)]
            for g, block in enumerate(pack(pieces)):
                b["pk"][g] = block.astype(BF16)

        def matrix_out(self, u):
            return local(self.b["pa"], self.param.at[self.mats(u)], self.b["loc"].at[2])

        def finish(self, u):
            kind, b = self.kind, self.b
            self.param_forward(u).wait()
            copy = local(self.param_land.at[u], b["pv"], b["loc"].at[3])
            copy.start()
            copy.wait()
            cut = kind.rows // 2
            for g in range(8):
                if g < 7:
                    quarters = [b["pv"][d, g].astype(F32)[:, :112] for d in range(4)]
                else:
                    quarters = [unpack([b["pv"][d, k].astype(F32) for k in range(7)])[7] for d in range(4)]
                b["pa"][g // 2, g % 2 * cut:(g % 2 + 1) * cut, :] = jnp.concatenate(quarters, axis=1).astype(BF16)
            self.matrix_out(u).start()

        def close(self, u):
            self.matrix_out(u).wait()

    stages = [LaneStage(kind) if kind.lanes else Stage(kind) for kind in kinds]
    bases = {}
    total_units = 0
    for k in ORDER:
        bases[k] = total_units
        total_units += kinds[k].units

    for k in ORDER:
        stage = stages[k]

        def send_all(u, carry, stage=stage):
            for copy in stage.exchange(u):
                copy.start()
            return carry

        lax.fori_loop(0, kinds[k].units, send_all, 0)

    def step(t, carry):
        def run(name, lag):
            for k in ORDER:
                method = getattr(stages[k], name, None)
                if method is None:
                    continue
                u = t - lag - bases[k]

                @pl.when((u >= 0) & (u < kinds[k].units))
                def _(method=method, u=u):
                    method(u)

        for name, lag in SCHEDULE:
            run(name, LAGS[lag])
        return carry

    lax.fori_loop(0, total_units + LAGS[-1], step, 0)


def solution(mesh):
    def local_step(*arrays):
        num = len(arrays) // 3
        kinds = [Kind(k, *arrays[k].shape[1:]) for k in range(num)]
        scratch = [kind.scratch() for kind in kinds]
        names = [tuple(shapes) for shapes in scratch]
        flat = [shape for shapes in scratch for shape in shapes.values()]
        flat.append(pltpu.VMEM((kinds[1].rows, kinds[1].rows), F32))
        row_shapes = [jax.ShapeDtypeStruct((kind.count, kind.q_rows, kind.q_cols), F32) for kind in kinds]
        full_shapes = [jax.ShapeDtypeStruct((kind.count, kind.rows, kind.cols), BF16) for kind in kinds]
        land_shapes = [jax.ShapeDtypeStruct((kind.count, 2, kind.q_rows, kind.q_cols), F32) for kind in kinds]
        far_shapes = list(row_shapes)
        lane = kinds[3]
        land_shapes[3] = jax.ShapeDtypeStruct((lane.count // 2, lane.rows, lane.cols), F32)
        far_shapes[3] = jax.ShapeDtypeStruct((lane.units, 7, lane.rows // 2, 128), F32)
        param_shape = jax.ShapeDtypeStruct((lane.units, 4, 7, lane.rows // 2, 128), BF16)
        flipped = [jnp.swapaxes(array, -1, -2) if kinds[i % num].flip else array for i, array in enumerate(arrays)]
        outs = pl.pallas_call(
            functools.partial(kernel, kinds, names),
            out_shape=row_shapes + row_shapes + full_shapes + land_shapes + far_shapes + [param_shape],
            in_specs=[pl.BlockSpec(memory_space=pl.ANY)] * (3 * num),
            out_specs=[pl.BlockSpec(memory_space=pl.ANY)] * (5 * num + 1),
            scratch_shapes=flat,
            compiler_params=pltpu.CompilerParams(
                collective_id=0, has_side_effects=True, vmem_limit_bytes=67043328
            ),
        )(*flipped)
        return tuple(jnp.swapaxes(array, -1, -2) if kinds[i % num].flip else array for i, array in enumerate(outs[:3 * num]))

    grad_spec = P(("stage", "data"), None, None, None)
    row_spec = P("stage", "data", None)
    full_spec = P("stage", None, None)
    in_specs = (grad_spec,) * 5 + (row_spec,) * 10
    out_specs = (row_spec,) * 10 + (full_spec,) * 5
    return jax.shard_map(local_step, mesh=mesh, in_specs=in_specs, out_specs=out_specs, check_vma=False)
```

time: 687 us -> 598 us (0.87)
  local copies, waits for them, and re-layouts: 97.8 us -> 43.9 us
  Pallas kernels: 586 us -> 552 us
    unnamed x47 -> x41, local copies, waits for them, and re-layouts: 97.8 us -> 43.9 us
    pallas_call x1, Pallas kernels: 586 us -> 552 us  [local_step(): pl.pallas_call(functools.partial(kernel, kinds, names), out_shape=row_sha...]
where the time goes in v2:
time: 598 us; the launch traced here: 597 us
  Pallas kernels  552 us (92%)
  local copies, waits for them, and re-layouts  43.9 us (7%)
    pallas_call x1, Pallas kernels, local_step(): pl.pallas_call(functools.partial(kernel, kinds, names), out_shape=row_sha...  552 us
    unnamed x41, local copies, waits for them, and re-layouts  43.9 us

profile of v2, /device:TPU:0, one launch (start us, length us, event | category | flops | bytes accessed | tf_op | source)
XLA Modules:
  0.0 596.5 jit_solution(1872701191617549804)
XLA Ops:
  0.7 551.9 %shard_map.262 = (f32[4,112,448]{2,1,0:T(8,128)}, f32[2,112,2560]{2,1,0:T(8,128)}, f32[1,448,640]{2,1,0:T(8,128)}, f32[32,320,112]{2,1,0:T(8,128)}, f32[16,80,44...) custom-call(f32[1,4,448,448]{3,2,1,0:T(8,128)} %refs_0_.1, ...), custom_call_target="tpu_custom_call" | custom-call | tf_op jit(solution)/shard_map/pallas_call | solution.py:677
  552.6 0.0 copy-start.7
  552.6 2.3 copy.45
  554.8 0.0 copy-start
  554.8 3.3 copy.46
  558.2 0.0 copy-done.7
  558.2 1.0 copy.47
  559.2 0.0 copy-done
  559.2 0.0 copy-start.2
  559.2 0.0 copy-start.8
  559.2 2.7 copy.48
  561.9 1.0 copy-done.2
  562.8 0.0 copy-start.4
  562.8 0.0 slice-start
  562.8 1.5 copy.49
  564.3 0.0 copy-done.8
  564.3 0.0 slice-start.1
  564.3 0.9 copy.50
  565.2 0.5 copy-done.4
  565.8 0.0 copy-start.6
  565.8 1.4 copy.51
  567.1 1.2 copy-done.6
  568.4 0.0 slice-start.2
  568.4 1.0 copy.52
  569.4 0.0 slice-done
  569.4 0.0 slice-done.1
  569.4 0.0 copy-start.1
  569.4 0.0 slice-start.3
  569.4 2.7 copy.53
  572.1 1.6 copy-done.1
  573.7 0.0 copy-start.5
  573.7 1.5 copy.54
  575.2 1.0 copy-done.5
  576.1 1.2 copy.55
  577.4 0.0 slice-done.2
  577.4 0.0 slice-done.3
  577.4 0.0 copy-start.3
  577.4 2.3 copy.56
  579.7 1.0 copy-done.3
  580.7 1.4 copy.57
  582.0 9.2 %copy.58 = bf16[32,448,320]{1,2,0:T(8,128)(2,1)} copy(bf16[32,448,320]{1,2,0:T(8,128)(2,1)} %bitcast.13) | data formatting | bytes 18350080
  591.2 5.3 copy.59
  (2 shorter events, 0.0 us)
Async XLA Ops:
  552.6 5.6 copy-start.7
  554.8 4.3 copy-start
  559.2 3.6 copy-start.2
  559.2 5.1 copy-start.8
  562.8 2.9 copy-start.4
  562.8 6.5 %slice-start = ((s8[5242880]{0:T(1024)(128)(4,1)}), s8[4194304]{0:T(1024)(128)(4,1)S(1)}, s32[]{:S(2)}) async-start(s8[5242880]{0:T(1024)(128)(4,1)} %bitcast.14), calls=%async_computation | async-start | bytes 8388608
  564.3 5.1 slice-start.1
  565.8 2.6 copy-start.6
  568.4 9.0 %slice-start.2 = ((s8[4587520]{0:T(1024)(128)(4,1)}), s8[4194304]{0:T(1024)(128)(4,1)S(1)}, s32[]{:S(2)}) async-start(s8[4587520]{0:T(1024)(128)(4,1)} %bitcast.20), calls=%async_computation.2 | async-start | bytes 8388608
  569.4 4.3 copy-start.1
  569.4 8.0 %slice-start.3 = ((s8[4587520]{0:T(1024)(128)(4,1)}), s8[393216]{0:T(1024)(128)(4,1)S(1)}, s32[]{:S(2)}) async-start(s8[4587520]{0:T(1024)(128)(4,1)} %bitcast.20), calls=%async_computation.3 | async-start | bytes 786432
  573.7 2.4 copy-start.5
  577.4 3.3 copy-start.3

commit v3 on v2

--- a/solution.py
+++ b/solution.py
@@ -19,13 +19,13 @@
 BF16 = jnp.bfloat16
 
 UNIT_MATS = (2, 2, 1, 4, 4)
-ORDER = (3, 2, 1, 0, 4)
-LAGS = (0, 2, 3, 4, 5, 6, 7, 8)
+ORDER = (4, 2, 1, 3, 0)
+LAGS = (0, 2, 4, 5, 6, 7, 8, 9)
 SCHEDULE = (
-    ("close", 7), ("finish", 6), ("forward", 5), ("combine", 1), ("start_matrix", 2),
+    ("combine", 1), ("start_matrix", 2), ("close", 7), ("drain", 5),
     ("load_weight_start", 4), ("first_loads", 0), ("second_loads", 1),
     ("start_start", 2), ("combine_start", 1),
-    ("iterate", 3), ("update", 4), ("iterate_start", 3), ("update_start", 4),
+    ("iterate", 3), ("finish", 6), ("forward", 5), ("update", 4), ("iterate_start", 3), ("update_start", 4),
     ("momentum", 1), ("partial", 0), ("norm_start", 1), ("partial_start", 0),
 )
 
@@ -38,6 +38,7 @@
         if self.flip:
             rows, cols = cols, rows
         self.lanes = index == 3
+        self.tail = index in (0, 4)
         self.count, self.rows, self.cols = count, rows, cols
         self.q_rows, self.q_cols = (rows, cols // 4) if self.flip else (rows // 4, cols)
         self.unit = UNIT_MATS[index]
@@ -45,6 +46,8 @@
         self.split = self.unit % 2 == 0
         self.half = self.unit // 2 if self.split else self.unit
         self.single = self.units == 1
+        self.pair = self.unit // 2
+        self.half_pair = self.half // 2 if self.tail else 0
         if index == 1:
             self.chunks = [(0, 1, 0, self.q_rows), (1, 1, 0, self.q_rows)]
         elif index == 2:
@@ -54,9 +57,9 @@
             self.chunks = [(0, self.unit, 0, self.q_rows)]
 
     def sems(self):
-        shapes = {name: pltpu.SemaphoreType.DMA((self.units, 3)) for name in (
+        shapes = {name: pltpu.SemaphoreType.DMA((self.units, 5)) for name in (
             "d2d_s", "d2d_r", "rs_s", "rs_r", "nm_s", "nm_r", "x_s", "x_r", "o_s", "o_r", "p_s", "p_r", "t_s", "t_r")}
-        shapes["loc"] = pltpu.SemaphoreType.DMA((10,))
+        shapes["loc"] = pltpu.SemaphoreType.DMA((14,))
         return shapes
 
     def scratch(self):
@@ -79,6 +82,15 @@
             shapes["dn"] = chunk
             shapes["w"] = pltpu.VMEM((unit, q_rows, q_cols), F32)
             shapes["pb"] = pltpu.VMEM((unit, q_rows, q_cols), BF16)
+        if self.tail:
+            shapes["st"] = pltpu.VMEM((slots, self.pair, q_rows, 128), F32)
+            shapes["xt"] = pltpu.VMEM((self.pair, q_rows, 128), F32)
+            shapes["pst"] = pltpu.VMEM((self.pair, q_rows, 128), BF16)
+            shapes["ptq"] = pltpu.VMEM((self.units, self.pair, q_rows, 128), BF16)
+            shapes["ptu"] = pltpu.VMEM((unit, q_rows, 64), BF16)
+        if self.half_pair:
+            shapes["xts"] = pltpu.VMEM((slots, 2, self.half_pair, q_rows, 128), BF16)
+            shapes["xtq"] = pltpu.VMEM((self.units, 2, self.half_pair, q_rows, 128), BF16)
         if self.split:
             shapes["orow"] = pltpu.VMEM((self.units, self.half, q_rows, q_cols), BF16)
         shapes.update(self.sems())
@@ -116,6 +128,10 @@
     return [jnp.concatenate([pieces[g], last[:, 16 * g:16 * g + 16]], axis=1) for g in range(7)]
 
 
+def join(left, right):
+    return jnp.concatenate([left[:, 384:448], right[:, 384:448]], axis=1)
+
+
 def unpack(blocks):
     return [block[:, :112] for block in blocks] + [jnp.concatenate([block[:, 112:128] for block in blocks], axis=1)]
 
@@ -173,7 +189,8 @@
     outs = refs[3 * num:8 * num]
     new_moms, new_masters, params, lands, far_lands = [outs[i * num:(i + 1) * num] for i in range(5)]
     param_land = refs[8 * num]
-    rest = list(refs[8 * num + 1:])
+    far_tails = {0: refs[8 * num + 1], 4: refs[8 * num + 2]}
+    rest = list(refs[8 * num + 3:])
     bufs = []
     for k in range(num):
         bufs.append({name: rest.pop(0) for name in names[k]})
@@ -212,6 +229,7 @@
             self.new_mom, self.new_master, self.param = new_moms[kind.index], new_masters[kind.index], params[kind.index]
             self.land, self.far_land = lands[kind.index], far_lands[kind.index]
             self.param_land = param_land
+            self.far_tail = far_tails.get(kind.index)
 
         def mats(self, u, offset=0, size=None):
             kind = self.kind
@@ -251,9 +269,14 @@
         def load_weight(self, u):
             return local(self.master.at[self.mats(u)], self.weight(), self.b["loc"].at[5])
 
-        def partial_send(self, u):
-            b = self.b
-            return remote(b["sb"].at[self.slot(u)], self.far_land.at[self.mats(u)], b["rs_s"].at[u, 0], b["rs_r"].at[u, 0], far_same)
+        def partial_sends(self, u):
+            b = self.b
+            src, dst = b["sb"].at[self.slot(u)], self.far_land.at[self.mats(u)]
+            pairs = [(src, dst)]
+            if self.kind.tail:
+                pairs = [(b["sb"].at[self.slot(u), :, :, 0:384], self.far_land.at[self.mats(u), :, 0:384]),
+                         (b["st"].at[self.slot(u)], self.far_tail.at[u])]
+            return [remote(src, dst, b["rs_s"].at[u, i], b["rs_r"].at[u, i], far_same) for i, (src, dst) in enumerate(pairs)]
 
         def first_loads(self, u):
             for i, copy in enumerate(self.exchange(u)):
@@ -272,9 +295,13 @@
                 for copy in copies:
                     copy.wait()
                 b["sb"][self.slot(u), mat:mat + nmat, row:row + nrow, :] = b["gf"][...] + b["df"][...]
+            if kind.tail:
+                for i in range(kind.pair):
+                    b["st"][self.slot(u), i] = join(b["sb"][self.slot(u), i], b["sb"][self.slot(u), i + kind.pair])
 
         def partial_start(self, u):
-            self.partial_send(u).start()
+            for copy in self.partial_sends(u):
+                copy.start()
 
         def second_loads(self, u):
             for copy in self.load_pair(u, self.kind.chunks[0], 1):
@@ -289,32 +316,46 @@
             ]
 
         def mom_out(self, u):
-            return local(self.b["mo"].at[self.slot(u)], self.new_mom.at[self.mats(u)], self.b["loc"].at[7])
+            return local(self.b["mo"].at[self.slot(u)], self.new_mom.at[self.mats(u)], self.b["loc"].at[12 + self.slot(u)])
 
         def momentum(self, u):
             kind, b = self.kind, self.b
             slot = self.slot(u)
-            self.partial_send(u).wait()
+            for copy in self.partial_sends(u):
+                copy.wait()
             self.load_mom(u).wait()
             near_g, near_d = ("gf", "df") if kind.single else ("gn", "dn")
             sums = [None] * kind.unit
             for index, chunk in enumerate(kind.chunks):
                 mat, nmat, row, nrow = chunk
-                far_copy = local(self.far_land.at[self.mats(u, mat, nmat), pl.ds(row, nrow), :], b["xl"], b["loc"].at[6])
-                far_copy.start()
+                if kind.tail:
+                    far_copies = [local(self.far_land.at[self.mats(u), :, 0:384], b["xl"].at[:, :, 0:384], b["loc"].at[6]),
+                                  local(self.far_tail.at[u], b["xt"], b["loc"].at[10])]
+                else:
+                    far_copies = [local(self.far_land.at[self.mats(u, mat, nmat), pl.ds(row, nrow), :], b["xl"], b["loc"].at[6])]
+                for copy in far_copies:
+                    copy.start()
                 copies = self.load_pair(u, chunk, 1)
                 if index:
                     for copy in copies:
                         copy.start()
                 for copy in copies:
                     copy.wait()
-                far_copy.wait()
+                for copy in far_copies:
+                    copy.wait()
                 for i in range(nmat):
-                    total = (b[near_g][i] + b[near_d][i]) + b["xl"][i]
-                    value = MOMENTUM * b["mo"][slot, mat + i, row:row + nrow, :] + total * 0.25
-                    b["mo"][slot, mat + i, row:row + nrow, :] = value
-                    sq_sum = jnp.sum(jnp.sum(value * value, axis=0, keepdims=True), axis=1, keepdims=True)
-                    sums[mat + i] = sq_sum if sums[mat + i] is None else sums[mat + i] + sq_sum
+                    if kind.tail:
+                        lane = i // kind.pair * 64
+                        cuts = ((slice(0, 384), b["xl"][i, :, 0:384]),
+                                (slice(384, 448), b["xt"][i % kind.pair][:, lane:lane + 64]))
+                    else:
+                        cuts = ((slice(0, kind.q_cols), b["xl"][i]),)
+                    for cut, far_sum in cuts:
+                        total = (b[near_g][i, :, cut] + b[near_d][i, :, cut]) + far_sum
+                        value = MOMENTUM * b["mo"][slot, mat + i, row:row + nrow, cut] + total * 0.25
+                        b["mo"][slot, mat + i, row:row + nrow, cut] = value
+                        sq_sum = jnp.sum(jnp.sum(value * value, axis=0, keepdims=True), axis=1, keepdims=True)
+                        sums[mat + i] = sq_sum if sums[mat + i] is None else sums[mat + i] + sq_sum
             for i in range(kind.unit):
                 b["nr"][u, me, i:i + 1, :] = jnp.broadcast_to(sums[i], (1, 128))
             self.mom_out(u).start()
@@ -330,10 +371,15 @@
             if kind.split:
                 mine = b["xs"].at[slot, pl.ds(core * kind.half, kind.half)]
                 theirs = b["xs"].at[slot, pl.ds(other * kind.half, kind.half)]
-                routes = ((theirs, partner), (mine, far_same), (theirs, far_other))
+                routes = [(theirs, place, partner), (mine, place, far_same), (theirs, place, far_other)]
             else:
-                routes = ((b["xs"].at[slot], partner), (b["xs"].at[slot], far_same))
-            return [remote(src, place, b["x_s"].at[u, i], b["x_r"].at[u, i], device) for i, (src, device) in enumerate(routes)]
+                routes = [(b["xs"].at[slot], place, partner), (b["xs"].at[slot], place, far_same)]
+            if kind.half_pair:
+                main = b["xg"].at[u, :, block_of(kind, me)[0], 0:384]
+                for h, base in enumerate((core * kind.half, other * kind.half)):
+                    routes[1 + h] = (b["xs"].at[slot, pl.ds(base, kind.half), :, 0:384], main, routes[1 + h][2])
+                routes += [(b["xts"].at[slot, h], b["xtq"].at[u, h], device) for h, device in enumerate((far_same, far_other))]
+            return [remote(src, dst, b["x_s"].at[u, i], b["x_r"].at[u, i], device) for i, (src, dst, device) in enumerate(routes)]
 
         def start_forward(self, u):
             kind, b = self.kind, self.b
@@ -353,6 +399,12 @@
                 b["xg"][(u, slice(None)) + block_of(kind, me)] = b["xs"][slot, pl.ds(core * kind.half, kind.half)]
             else:
                 b["xg"][(u, slice(None)) + block_of(kind, me)] = b["xs"][slot]
+            if kind.half_pair:
+                for h, base in enumerate((core * kind.half, other * kind.half)):
+                    for i in range(kind.half_pair):
+                        left = b["xs"][slot, base + i].astype(F32)
+                        right = b["xs"][slot, base + i + kind.half_pair].astype(F32)
+                        b["xts"][slot, h, i] = join(left, right).astype(BF16)
             self.mom_out(u).wait()
 
         def start_start(self, u):
@@ -370,6 +422,14 @@
                 forward = self.start_forward(u)
                 forward.start()
                 forward.wait()
+            if self.kind.half_pair:
+                kind, b = self.kind, self.b
+                for h, device in enumerate((far_same, far_other)):
+                    for i in range(kind.half_pair):
+                        both = b["xtq"][u, h, i].astype(F32)
+                        for side in range(2):
+                            part = both[:, 64 * side:64 * side + 64].astype(BF16)
+                            b["xg"][u, i + side * kind.half_pair, block_of(kind, device)[0], 384:448] = part
             newton_schulz(self.kind, self.b["xg"], u, gram_acc)
 
         def iterate_start(self, u):
@@ -385,15 +445,26 @@
         def param_sends(self, u):
             kind, b = self.kind, self.b
             place = self.param.at[(self.mats(u),) + block_of(kind, me)]
-            return [
-                remote(self.rounded(), place, b["p_s"].at[u, i], b["p_r"].at[u, i], device)
-                for i, device in enumerate((partner, far_same))
-            ]
-
-        def param_forward(self, u):
+            routes = [(self.rounded(), place, partner, 0), (self.rounded(), place, far_same, 1)]
+            if kind.tail:
+                main = self.param.at[self.mats(u), block_of(kind, me)[0], 0:384]
+                routes[1:] = [(b["pb"].at[:, :, 0:384], main, far_same, 1), (b["pst"], b["ptq"].at[u], far_same, 3)]
+            return [remote(src, dst, b["p_s"].at[u, i], b["p_r"].at[u, i], device) for src, dst, device, i in routes]
+
+        def param_forwards(self, u):
             kind, b = self.kind, self.b
             place = self.param.at[(self.mats(u),) + block_of(kind, far_same)]
-            return remote(place, place, b["p_s"].at[u, 2], b["p_r"].at[u, 2], partner)
+            routes = [(place, place, 2)]
+            if kind.tail:
+                main = self.param.at[self.mats(u), block_of(kind, far_same)[0], 0:384]
+                routes = [(main, main, 2), (b["ptu"], self.tail_place(u), 4)]
+            return [remote(src, dst, b["p_s"].at[u, i], b["p_r"].at[u, i], partner) for src, dst, i in routes]
+
+        def tail_place(self, u):
+            return self.param.at[self.mats(u), block_of(self.kind, far_same)[0], 384:448]
+
+        def tail_out(self, u):
+            return local(self.b["ptu"], self.tail_place(u), self.b["loc"].at[11])
 
         def update(self, u):
             kind, b = self.kind, self.b
@@ -411,6 +482,9 @@
                     new = old - LEARN_RATE * (kind.scale * ortho(j).astype(F32) + WEIGHT_DECAY * old)
                     weight[base + j] = new
                     self.rounded()[base + j] = new.astype(BF16)
+            if kind.tail:
+                for i in range(kind.pair):
+                    b["pst"][i] = join(b["pb"][i].astype(F32), b["pb"][i + kind.pair].astype(F32)).astype(BF16)
 
         def update_start(self, u):
             self.weight_out(u).start()
@@ -418,15 +492,27 @@
             for copy in self.param_sends(u):
                 copy.start()
 
+        def drain(self, u):
+            self.weight_out(u).wait()
+
         def forward(self, u):
-            self.weight_out(u).wait()
             self.param_out(u).wait()
             for copy in self.param_sends(u):
                 copy.wait()
-            self.param_forward(u).start()
+            kind, b = self.kind, self.b
+            if kind.tail:
+                for i in range(kind.unit):
+                    lane = i // kind.pair * 64
+                    b["ptu"][i] = b["ptq"][u, i % kind.pair].astype(F32)[:, lane:lane + 64].astype(BF16)
+                self.tail_out(u).start()
+            for copy in self.param_forwards(u):
+                copy.start()
 
         def finish(self, u):
-            self.param_forward(u).wait()
+            if self.kind.tail:
+                self.tail_out(u).wait()
+            for copy in self.param_forwards(u):
+                copy.wait()
 
         def load_weight_start(self, u):
             self.load_weight(u).start()
@@ -471,9 +557,9 @@
                 piece = far_piece(g // 4, g // 2 % 2, g % 2)
                 b["sb"][slot, g] = jnp.concatenate([piece, last[:, 16 * g:16 * g + 16]], axis=1)
 
-        def partial_send(self, u):
-            b = self.b
-            return remote(b["sb"].at[self.slot(u)], self.far_land.at[u], b["rs_s"].at[u, 0], b["rs_r"].at[u, 0], far_same)
+        def partial_sends(self, u):
+            b = self.b
+            return [remote(b["sb"].at[self.slot(u)], self.far_land.at[u], b["rs_s"].at[u, 0], b["rs_r"].at[u, 0], far_same)]
 
         def second_loads(self, u):
             self.load_mom(u).start()
@@ -481,7 +567,8 @@
         def combine(self, u):
             kind, b = self.kind, self.b
             slot = self.slot(u)
-            self.partial_send(u).wait()
+            for copy in self.partial_sends(u):
+                copy.wait()
             copy = local(self.far_land.at[u], b["xl"], b["loc"].at[6])
             copy.start()
             copy.wait()
@@ -577,10 +664,10 @@
                 for i, device in enumerate((partner, far_same))
             ]
 
-        def param_forward(self, u):
+        def param_forwards(self, u):
             b = self.b
             place = self.param_land.at[u, far_same]
-            return remote(place, place, b["p_s"].at[u, 2], b["p_r"].at[u, 2], partner)
+            return [remote(place, place, b["p_s"].at[u, 2], b["p_r"].at[u, 2], partner)]
 
         def update(self, u):
             kind, b = self.kind, self.b
@@ -605,7 +692,8 @@
 
         def finish(self, u):
             kind, b = self.kind, self.b
-            self.param_forward(u).wait()
+            for copy in self.param_forwards(u):
+                copy.wait()
             copy = local(self.param_land.at[u], b["pv"], b["loc"].at[3])
             copy.start()
             copy.wait()
@@ -673,12 +761,13 @@
         land_shapes[3] = jax.ShapeDtypeStruct((lane.count // 2, lane.rows, lane.cols), F32)
         far_shapes[3] = jax.ShapeDtypeStruct((lane.units, 7, lane.rows // 2, 128), F32)
         param_shape = jax.ShapeDtypeStruct((lane.units, 4, 7, lane.rows // 2, 128), BF16)
+        tail_shapes = [jax.ShapeDtypeStruct((kind.units, kind.pair, kind.q_rows, 128), F32) for kind in kinds if kind.tail]
         flipped = [jnp.swapaxes(array, -1, -2) if kinds[i % num].flip else array for i, array in enumerate(arrays)]
         outs = pl.pallas_call(
             functools.partial(kernel, kinds, names),
-            out_shape=row_shapes + row_shapes + full_shapes + land_shapes + far_shapes + [param_shape],
+            out_shape=row_shapes + row_shapes + full_shapes + land_shapes + far_shapes + [param_shape] + tail_shapes,
             in_specs=[pl.BlockSpec(memory_space=pl.ANY)] * (3 * num),
-            out_specs=[pl.BlockSpec(memory_space=pl.ANY)] * (5 * num + 1),
+            out_specs=[pl.BlockSpec(memory_space=pl.ANY)] * (5 * num + 3),
             scratch_shapes=flat,
             compiler_params=pltpu.CompilerParams(
                 collective_id=0, has_side_effects=True, vmem_limit_bytes=67043328

time: 598 us -> 556 us (0.930)
  Pallas kernels: 552 us -> 510 us
    pallas_call x1, Pallas kernels: 552 us -> 510 us  [local_step(): pl.pallas_call(functools.partial(kernel, kinds, names), out_shape=row_sha...]
where the time goes in v3:
time: 556 us; the launch traced here: 555 us
  Pallas kernels  510 us (92%)
  local copies, waits for them, and re-layouts  43.9 us (8%)
    pallas_call x1, Pallas kernels, local_step(): pl.pallas_call(functools.partial(kernel, kinds, names), out_shape=row_sha...  510 us
    unnamed x41, local copies, waits for them, and re-layouts  43.9 us

profile of v3, /device:TPU:0, one launch (start us, length us, event | category | flops | bytes accessed | tf_op | source)
XLA Modules:
  0.0 555.0 jit_solution(15039263655579080589)
XLA Ops:
  0.7 510.4 %shard_map.262 = (f32[4,112,448]{2,1,0:T(8,128)}, f32[2,112,2560]{2,1,0:T(8,128)}, f32[1,448,640]{2,1,0:T(8,128)}, f32[32,320,112]{2,1,0:T(8,128)}, f32[16,80,44...) custom-call(f32[1,4,448,448]{3,2,1,0:T(8,128)} %refs_0_.1, ...), custom_call_target="tpu_custom_call" | custom-call | tf_op jit(solution)/shard_map/pallas_call | solution.py:766
  511.0 0.0 copy-start.7
  511.1 2.3 copy.45
  513.3 0.0 copy-start
  513.3 3.3 copy.46
  516.6 0.0 copy-done.7
  516.6 1.0 copy.47
  517.7 0.0 copy-done
  517.7 0.0 copy-start.2
  517.7 0.0 copy-start.8
  517.7 2.7 copy.48
  520.3 1.0 copy-done.2
  521.3 0.0 copy-start.4
  521.3 0.0 slice-start
  521.3 1.5 copy.49
  522.8 0.0 copy-done.8
  522.8 0.0 slice-start.1
  522.8 0.9 copy.50
  523.7 0.5 copy-done.4
  524.2 0.0 copy-start.6
  524.2 1.4 copy.51
  525.6 1.2 copy-done.6
  526.8 0.0 slice-start.2
  526.8 1.0 copy.52
  527.8 0.0 slice-done
  527.8 0.0 slice-done.1
  527.8 0.0 copy-start.1
  527.8 0.0 slice-start.3
  527.9 2.7 copy.53
  530.5 1.6 copy-done.1
  532.1 0.0 copy-start.5
  532.1 1.5 copy.54
  533.6 1.0 copy-done.5
  534.6 1.2 copy.55
  535.8 0.0 slice-done.2
  535.8 0.0 slice-done.3
  535.8 0.0 copy-start.3
  535.8 2.3 copy.56
  538.2 1.0 copy-done.3
  539.1 1.4 copy.57
  540.5 9.2 %copy.58 = bf16[32,448,320]{1,2,0:T(8,128)(2,1)} copy(bf16[32,448,320]{1,2,0:T(8,128)(2,1)} %bitcast.13) | data formatting | bytes 18350080
  549.7 5.3 copy.59
  (2 shorter events, 0.0 us)
Async XLA Ops:
  511.0 5.6 %copy-start.7 = (f32[1,448,640]{2,1,0:T(8,128)S(1)}, f32[1,448,640]{2,1,0:T(8,128)}, u32[]{:S(2)}) copy-start(f32[1,448,640]{2,1,0:T(8,128)} %get-tuple-element.32) | copy-start | bytes 3440644
  513.3 4.3 copy-start
  517.7 3.6 copy-start.2
  517.7 5.1 copy-start.8
  521.3 2.9 copy-start.4
  521.3 6.5 %slice-start = ((s8[5242880]{0:T(1024)(128)(4,1)}), s8[4194304]{0:T(1024)(128)(4,1)S(1)}, s32[]{:S(2)}) async-start(s8[5242880]{0:T(1024)(128)(4,1)} %bitcast.14), calls=%async_computation | async-start | bytes 8388608
  522.8 5.1 slice-start.1
  524.2 2.6 copy-start.6
  526.8 9.0 %slice-start.2 = ((s8[4587520]{0:T(1024)(128)(4,1)}), s8[4194304]{0:T(1024)(128)(4,1)S(1)}, s32[]{:S(2)}) async-start(s8[4587520]{0:T(1024)(128)(4,1)} %bitcast.20), calls=%async_computation.2 | async-start | bytes 8388608
  527.8 4.3 copy-start.1
  527.8 8.0 %slice-start.3 = ((s8[4587520]{0:T(1024)(128)(4,1)}), s8[393216]{0:T(1024)(128)(4,1)S(1)}, s32[]{:S(2)}) async-start(s8[4587520]{0:T(1024)(128)(4,1)} %bitcast.20), calls=%async_computation.3 | async-start | bytes 786432
  532.1 2.4 copy-start.5
  535.8 3.3 copy-start.3

commit v4 on v3

--- a/solution.py
+++ b/solution.py
@@ -46,6 +46,7 @@
         self.split = self.unit % 2 == 0
         self.half = self.unit // 2 if self.split else self.unit
         self.single = self.units == 1
+        self.late = index == 1
         self.pair = self.unit // 2
         self.half_pair = self.half // 2 if self.tail else 0
         if index == 1:
@@ -440,10 +441,14 @@
             return local(self.weight(), self.new_master.at[self.mats(u)], self.b["loc"].at[8])
 
         def param_out(self, u):
+            if self.kind.late:
+                return local(self.rounded(), self.param.at[self.mats(u)], self.b["loc"].at[9])
             return local(self.rounded(), self.param.at[(self.mats(u),) + block_of(self.kind, me)], self.b["loc"].at[9])
 
         def param_sends(self, u):
             kind, b = self.kind, self.b
+            if kind.late:
+                return []
             place = self.param.at[(self.mats(u),) + block_of(kind, me)]
             routes = [(self.rounded(), place, partner, 0), (self.rounded(), place, far_same, 1)]
             if kind.tail:
@@ -453,6 +458,8 @@
 
         def param_forwards(self, u):
             kind, b = self.kind, self.b
+            if kind.late:
+                return []
             place = self.param.at[(self.mats(u),) + block_of(kind, far_same)]
             routes = [(place, place, 2)]
             if kind.tail:
@@ -745,6 +752,76 @@
     lax.fori_loop(0, total_units + LAGS[-1], step, 0)
 
 
+def copy_kernel(cuts, num, *refs):
+    sources, targets, stores = refs[:num], refs[num:2 * num], refs[2 * num:3 * num]
+    in_sem, out_sem = refs[3 * num:]
+    loads = [pltpu.make_async_copy(sources[i].at[pl.ds(lo, size)], stores[i].at[pl.ds(lo, size)], in_sem.at[n])
+             for n, (i, lo, size) in enumerate(cuts)]
+    saves = [pltpu.make_async_copy(stores[i].at[pl.ds(lo, size)], targets[i].at[pl.ds(lo, size)], out_sem.at[n])
+             for n, (i, lo, size) in enumerate(cuts)]
+    for load in loads:
+        load.start()
+    for load, save in zip(loads, saves):
+        load.wait()
+        save.start()
+    for save in saves:
+        save.wait()
+
+
+def copy_out(arrays, pieces):
+    cuts = []
+    for i, array in enumerate(arrays):
+        size = max(1, array.shape[0] // pieces)
+        cuts += [(i, lo, size) for lo in range(0, array.shape[0], size)]
+    total = sum(array.size * array.dtype.itemsize for array in arrays)
+    return pl.pallas_call(
+        functools.partial(copy_kernel, cuts, len(arrays)),
+        out_shape=[jax.ShapeDtypeStruct(array.shape, array.dtype) for array in arrays],
+        in_specs=[pl.BlockSpec(memory_space=pl.ANY)] * len(arrays),
+        out_specs=[pl.BlockSpec(memory_space=pl.ANY)] * len(arrays),
+        scratch_shapes=[pltpu.VMEM(array.shape, array.dtype) for array in arrays]
+        + [pltpu.SemaphoreType.DMA((len(cuts),))] * 2,
+        compiler_params=pltpu.CompilerParams(vmem_limit_bytes=67043328),
+        cost_estimate=pl.CostEstimate(flops=1200 * total, bytes_accessed=2 * total, transcendentals=0),
+    )(*arrays)
+
+
+def gather_kernel(own, far, near, near_far, target, *rest):
+    stores, sem = rest[:4], rest[4]
+    me = lax.axis_index("data")
+    chip, core = me // 2, me % 2
+    places = (me, 2 * (1 - chip) + core, 2 * chip + 1 - core, 2 * (1 - chip) + 1 - core)
+    rows = own.shape[1]
+    loads = [pltpu.make_async_copy(source, stores[i], sem.at[0, i]) for i, source in enumerate((own, far, near, near_far))]
+    saves = [pltpu.make_async_copy(stores[i], target.at[:, pl.ds(pl.multiple_of(place * rows, 16), rows), :], sem.at[1, i])
+             for i, place in enumerate(places)]
+    for load in loads:
+        load.start()
+    for load, save in zip(loads, saves):
+        load.wait()
+        save.start()
+    for save in saves:
+        save.wait()
+
+
+def gather_rows(own, arrays):
+    far = lax.ppermute(own, "data", [(0, 2), (2, 0), (1, 3), (3, 1)])
+    cores = [(0, 1), (1, 0), (2, 3), (3, 2)]
+    near = lax.ppermute(own, "data", cores)
+    copied = copy_out(arrays, 4)
+    far, near, copied = lax.optimization_barrier((far, near, copied))
+    near_far = lax.ppermute(far, "data", cores)
+    gathered = pl.pallas_call(
+        gather_kernel,
+        out_shape=jax.ShapeDtypeStruct((own.shape[0], 4 * own.shape[1], own.shape[2]), own.dtype),
+        in_specs=[pl.BlockSpec(memory_space=pl.ANY)] * 4,
+        out_specs=pl.BlockSpec(memory_space=pl.ANY),
+        scratch_shapes=[pltpu.VMEM(own.shape, own.dtype)] * 4 + [pltpu.SemaphoreType.DMA((2, 4))],
+        cost_estimate=pl.CostEstimate(flops=0, bytes_accessed=8 * own.size * 2, transcendentals=0),
+    )(own, far, near, near_far)
+    return gathered, copied
+
+
 def solution(mesh):
     def local_step(*arrays):
         num = len(arrays) // 3
@@ -754,7 +831,10 @@
         flat = [shape for shapes in scratch for shape in shapes.values()]
         flat.append(pltpu.VMEM((kinds[1].rows, kinds[1].rows), F32))
         row_shapes = [jax.ShapeDtypeStruct((kind.count, kind.q_rows, kind.q_cols), F32) for kind in kinds]
-        full_shapes = [jax.ShapeDtypeStruct((kind.count, kind.rows, kind.cols), BF16) for kind in kinds]
+        full_shapes = [
+            jax.ShapeDtypeStruct((kind.count,) + ((kind.q_rows, kind.q_cols) if kind.late else (kind.rows, kind.cols)), BF16)
+            for kind in kinds
+        ]
         land_shapes = [jax.ShapeDtypeStruct((kind.count, 2, kind.q_rows, kind.q_cols), F32) for kind in kinds]
         far_shapes = list(row_shapes)
         lane = kinds[3]
@@ -773,6 +853,12 @@
                 collective_id=0, has_side_effects=True, vmem_limit_bytes=67043328
             ),
         )(*flipped)
+        outs = list(outs[:3 * num])
+        late = next(2 * num + kind.index for kind in kinds if kind.late)
+        early = [i for i in range(3 * num) if i != late]
+        gathered, copied = gather_rows(outs[late], [outs[i] for i in early])
+        for i, array in zip(early + [late], list(copied) + [gathered]):
+            outs[i] = array
         return tuple(jnp.swapaxes(array, -1, -2) if kinds[i % num].flip else array for i, array in enumerate(outs[:3 * num]))
 
     grad_spec = P(("stage", "data"), None, None, None)

time: 556 us -> 527 us (0.948)
  local copies, waits for them, and re-layouts: 43.9 us -> 0.99 us
  Pallas kernels: 510 us -> 520 us
    unnamed x41 -> x2, local copies, waits for them, and re-layouts: 43.9 us -> 0.99 us
    pallas_call x0 -> x2, Pallas kernels: none -> 34.2 us  [the longest x1 30.6 us: copy_out(): pl.pallas_call(functools.partial(copy_kernel, cuts, len(arrays)), out_sha...]
    pallas_call x1, Pallas kernels: 510 us -> 486 us  [local_step(): pl.pallas_call(functools.partial(kernel, kinds, names), out_shape=row_sha...]
  transfers between devices with their start and end apart: 0 -> 3, of which waited for: 0 -> 1; matrix products, arithmetic and copies ran while one was open for 0% -> 0% of each run, Pallas kernels for 0% -> 6%
where the time goes in v4:
time: 527 us; the launch traced here: 526 us
  Pallas kernels  520 us (99%)
    pallas_call x1, Pallas kernels, local_step(): pl.pallas_call(functools.partial(kernel, kinds, names), out_shape=row_sha...  486 us
    pallas_call x1, Pallas kernels, copy_out(): pl.pallas_call(functools.partial(copy_kernel, cuts, len(arrays)), out_sha...  30.6 us
  transfers between devices with their start and end apart: 3, of which 1 were waited for; matrix products, arithmetic and copies ran while one was open for 0% of the time, Pallas kernels for 6%

profile of v4, /device:TPU:0, one launch (start us, length us, event | category | flops | bytes accessed | tf_op | source)
XLA Modules:
  0.0 525.9 jit_solution(13351081864969584902)
XLA Ops:
  0.7 485.7 %shard_map.262 = (f32[4,112,448]{2,1,0:T(8,128)}, f32[2,112,2560]{2,1,0:T(8,128)}, f32[1,448,640]{2,1,0:T(8,128)}, f32[32,320,112]{2,1,0:T(8,128)}, f32[16,80,44...) custom-call(f32[1,4,448,448]{3,2,1,0:T(8,128)} %refs_0_.1, ...), custom_call_target="tpu_custom_call" | custom-call | tf_op jit(solution)/shard_map/pallas_call | solution.py:846
  486.3 0.0 collective-permute-start.1
  486.4 1.3 collective-permute-start
  487.6 30.6 %shard_map.263 = (f32[4,112,448]{2,1,0:T(8,128)}, f32[2,112,2560]{2,1,0:T(8,128)}, f32[1,448,640]{2,1,0:T(8,128)}, f32[32,320,112]{2,1,0:T(8,128)}, f32[16,80,44...) custom-call(f32[4,112,448]{2,1,0:T(8,128)} %get-tuple-element.61.ref, ...), custom_call_target="tpu_custom_call" | custom-call | flops 47893708800 | bytes 79822848 | tf_op jit(solution)/shard_map/pallas_call | solution.py:777
  518.2 0.0 collective-permute-done.1.near
  518.3 0.0 collective-permute-done.far
  518.3 0.2 collective-permute-start.2
  518.5 2.6 collective-permute-done.2.near_far
  521.1 0.0 copy-start
  521.1 1.0 copy-done
  522.1 3.6 shard_map.264
Async XLA Ops:
  486.3 31.9 %collective-permute-start.1 = (bf16[2,112,2560]{2,1,0:T(8,128)(2,1)}, bf16[2,112,2560]{2,1,0:T(8,128)(2,1)}, u32[]{:S(2)}, u32[]{:S(2)}) collective-permute-start(bf16[2,112,2560]{2,1,0:T(8,128)(2,1)} %get-tuple-element.60.own), channel_id=1, source_target_pairs={{0,1},{1,0},{2,3},{3,2},{4,5},{5,4},{6,7},{7,6}} | collective-permute-start | bytes 3440648 | tf_op jit(solution)/shard_map/ppermute | solution.py:810
  486.4 31.9 %collective-permute-start = (bf16[2,112,2560]{2,1,0:T(8,128)(2,1)}, bf16[2,112,2560]{2,1,0:T(8,128)(2,1)}, u32[]{:S(2)}, u32[]{:S(2)}) collective-permute-start(bf16[2,112,2560]{2,1,0:T(8,128)(2,1)} %get-tuple-element.60.own), channel_id=1, source_target_pairs={{0,2},{2,0},{1,3},{3,1},{4,6},{6,4},{5,7},{7,5}} | collective-permute-start | bytes 3440648 | tf_op jit(solution)/shard_map/ppermute | solution.py:808
  518.3 2.8 collective-permute-start.2
  521.1 1.0 copy-start

commit v5 on v4

--- a/solution.py
+++ b/solution.py
@@ -20,14 +20,16 @@
 
 UNIT_MATS = (2, 2, 1, 4, 4)
 ORDER = (4, 2, 1, 3, 0)
-LAGS = (0, 2, 4, 5, 6, 7, 8, 9)
+LANE, MAIN, TAIL, BLOCK, PAD = 128, 384, 64, 112, 16
+UPDATE = 9
 SCHEDULE = (
-    ("combine", 1), ("start_matrix", 2), ("close", 7), ("drain", 5),
-    ("load_weight_start", 4), ("first_loads", 0), ("second_loads", 1),
-    ("start_start", 2), ("combine_start", 1),
-    ("iterate", 3), ("finish", 6), ("forward", 5), ("update", 4), ("iterate_start", 3), ("update_start", 4),
-    ("momentum", 1), ("partial", 0), ("norm_start", 1), ("partial_start", 0),
+    ("exchange_start", 0), ("combine", 4), ("start_matrix", 6), ("close", UPDATE + 3), ("drain", UPDATE + 1),
+    ("load_weight_start", UPDATE), ("first_loads", 2), ("second_loads", 4),
+    ("start_start", 6), ("combine_start", 4), ("momentum", 4), ("norm_start", 4),
+    ("partial", 2), ("iterate", 7), ("partial_start", 2), ("iterate_start", 7),
+    ("update", UPDATE), ("update_start", UPDATE), ("finish", UPDATE + 2), ("forward", UPDATE + 1),
 )
+STEPS_BEHIND = max(lag for _, lag in SCHEDULE)
 
 
 class Kind:
@@ -60,7 +62,7 @@
     def sems(self):
         shapes = {name: pltpu.SemaphoreType.DMA((self.units, 5)) for name in (
             "d2d_s", "d2d_r", "rs_s", "rs_r", "nm_s", "nm_r", "x_s", "x_r", "o_s", "o_r", "p_s", "p_r", "t_s", "t_r")}
-        shapes["loc"] = pltpu.SemaphoreType.DMA((14,))
+        shapes["loc"] = pltpu.SemaphoreType.DMA((16,))
         return shapes
 
     def scratch(self):
@@ -76,22 +78,22 @@
             sb=pltpu.VMEM((slots, unit, q_rows, q_cols), F32),
             xs=pltpu.VMEM((slots, unit, q_rows, q_cols), BF16),
             xg=pltpu.VMEM((self.units, self.half, self.rows, self.cols), BF16),
-            nr=pltpu.VMEM((self.units, 4, 8, 128), F32),
+            nr=pltpu.VMEM((self.units, 4, 8, LANE), F32),
         )
         if not self.single:
             shapes["gn"] = chunk
             shapes["dn"] = chunk
             shapes["w"] = pltpu.VMEM((unit, q_rows, q_cols), F32)
-            shapes["pb"] = pltpu.VMEM((unit, q_rows, q_cols), BF16)
+            shapes["pb"] = pltpu.VMEM((2, unit, q_rows, q_cols), BF16)
         if self.tail:
-            shapes["st"] = pltpu.VMEM((slots, self.pair, q_rows, 128), F32)
-            shapes["xt"] = pltpu.VMEM((self.pair, q_rows, 128), F32)
-            shapes["pst"] = pltpu.VMEM((self.pair, q_rows, 128), BF16)
-            shapes["ptq"] = pltpu.VMEM((self.units, self.pair, q_rows, 128), BF16)
-            shapes["ptu"] = pltpu.VMEM((unit, q_rows, 64), BF16)
+            shapes["st"] = pltpu.VMEM((slots, self.pair, q_rows, LANE), F32)
+            shapes["xt"] = pltpu.VMEM((self.pair, q_rows, LANE), F32)
+            shapes["pst"] = pltpu.VMEM((2, self.pair, q_rows, LANE), BF16)
+            shapes["ptq"] = pltpu.VMEM((self.units, self.pair, q_rows, LANE), BF16)
+            shapes["ptu"] = pltpu.VMEM((unit, q_rows, TAIL), BF16)
         if self.half_pair:
-            shapes["xts"] = pltpu.VMEM((slots, 2, self.half_pair, q_rows, 128), BF16)
-            shapes["xtq"] = pltpu.VMEM((self.units, 2, self.half_pair, q_rows, 128), BF16)
+            shapes["xts"] = pltpu.VMEM((slots, 2, self.half_pair, q_rows, LANE), BF16)
+            shapes["xtq"] = pltpu.VMEM((self.units, 2, self.half_pair, q_rows, LANE), BF16)
         if self.split:
             shapes["orow"] = pltpu.VMEM((self.units, self.half, q_rows, q_cols), BF16)
         shapes.update(self.sems())
@@ -102,23 +104,23 @@
         shapes = dict(
             gf=pltpu.VMEM((half, rows, cols), F32),
             df=pltpu.VMEM((half, rows, cols), F32),
-            sb=pltpu.VMEM((2, 7, rows // 2, 128), F32),
+            sb=pltpu.VMEM((2, 7, rows // 2, LANE), F32),
             nb=pltpu.VMEM((2, 2, half, rows, lanes), F32),
-            xl=pltpu.VMEM((7, rows // 2, 128), F32),
+            xl=pltpu.VMEM((7, rows // 2, LANE), F32),
             tq=pltpu.VMEM((half, rows, lanes), F32),
             tr=pltpu.VMEM((units, half, rows, lanes), F32),
             mo=pltpu.VMEM((2, unit, rows, lanes), F32),
             w=pltpu.VMEM((unit, rows, lanes), F32),
-            xs=pltpu.VMEM((2, unit, rows, 128), BF16),
-            xp=pltpu.VMEM((2, 2, 7, rows // 4, 128), BF16),
-            xq=pltpu.VMEM((units, 2, 7, rows // 4, 128), BF16),
+            xs=pltpu.VMEM((2, unit, rows, LANE), BF16),
+            xp=pltpu.VMEM((2, 2, 7, rows // 4, LANE), BF16),
+            xq=pltpu.VMEM((units, 2, 7, rows // 4, LANE), BF16),
             xg=pltpu.VMEM((units, half, rows, 512), BF16),
-            orow=pltpu.VMEM((units, half, rows, 128), BF16),
+            orow=pltpu.VMEM((units, half, rows, LANE), BF16),
             pb=pltpu.VMEM((unit, rows, lanes), BF16),
-            pk=pltpu.VMEM((7, rows // 2, 128), BF16),
-            pv=pltpu.VMEM((4, 7, rows // 2, 128), BF16),
+            pk=pltpu.VMEM((2, 7, rows // 2, LANE), BF16),
+            pv=pltpu.VMEM((4, 7, rows // 2, LANE), BF16),
             pa=pltpu.VMEM((unit, rows, cols), BF16),
-            nr=pltpu.VMEM((units, 4, 8, 128), F32),
+            nr=pltpu.VMEM((units, 4, 8, LANE), F32),
         )
         shapes.update(self.sems())
         return shapes
@@ -130,11 +132,11 @@
 
 
 def join(left, right):
-    return jnp.concatenate([left[:, 384:448], right[:, 384:448]], axis=1)
+    return jnp.concatenate([left[:, MAIN:MAIN + TAIL], right[:, MAIN:MAIN + TAIL]], axis=1)
 
 
 def unpack(blocks):
-    return [block[:, :112] for block in blocks] + [jnp.concatenate([block[:, 112:128] for block in blocks], axis=1)]
+    return [block[:, :BLOCK] for block in blocks] + [jnp.concatenate([block[:, BLOCK:LANE] for block in blocks], axis=1)]
 
 
 def dot(left, right, dims):
@@ -174,11 +176,11 @@
     else:
 
         def iteration(_, carry):
-            for j in range(kind.half):
-                mat = xg[u, j]
-                gram_mat = dot(mat, mat, ((1,), (1,))).astype(BF16)
-                update = dot(poly(gram_mat), mat, ((1,), (0,)))
-                xg[u, j] = (COEF_A * mat.astype(F32) + update).astype(BF16)
+            mats = [xg[u, j] for j in range(kind.half)]
+            polys = [poly(gram_mat) for gram_mat in [dot(mat, mat, ((1,), (1,))).astype(BF16) for mat in mats]]
+            news = [COEF_A * mat.astype(F32) + dot(poly_mat, mat, ((1,), (0,))) for poly_mat, mat in zip(polys, mats)]
+            for j, new in enumerate(news):
+                xg[u, j] = new.astype(BF16)
             return carry
 
     lax.fori_loop(0, NS_STEPS, iteration, 0)
@@ -219,7 +221,7 @@
     def block_of(kind, device, row=0, nrow=None):
         nrow = kind.q_rows if nrow is None else nrow
         if kind.flip:
-            return pl.ds(row, nrow), pl.ds(pl.multiple_of(device * kind.q_cols, 128), kind.q_cols)
+            return pl.ds(row, nrow), pl.ds(pl.multiple_of(device * kind.q_cols, LANE), kind.q_cols)
         return pl.ds(pl.multiple_of(device * kind.q_rows + row, 16), nrow), slice(None)
 
     class Stage:
@@ -248,6 +250,10 @@
                 for i, quarter in enumerate((far_other, partner))
             ]
 
+        def exchange_start(self, u):
+            for copy in self.exchange(u):
+                copy.start()
+
         def load_pair(self, u, chunk, which):
             kind, b = self.kind, self.b
             mat, nmat, row, nrow = chunk
@@ -264,8 +270,8 @@
         def weight(self):
             return self.b["sb"].at[0] if self.kind.single else self.b["w"]
 
-        def rounded(self):
-            return self.b["xs"].at[0] if self.kind.single else self.b["pb"]
+        def rounded(self, u):
+            return self.b["xs"].at[0] if self.kind.single else self.b["pb"].at[self.slot(u)]
 
         def load_weight(self, u):
             return local(self.master.at[self.mats(u)], self.weight(), self.b["loc"].at[5])
@@ -275,7 +281,7 @@
             src, dst = b["sb"].at[self.slot(u)], self.far_land.at[self.mats(u)]
             pairs = [(src, dst)]
             if self.kind.tail:
-                pairs = [(b["sb"].at[self.slot(u), :, :, 0:384], self.far_land.at[self.mats(u), :, 0:384]),
+                pairs = [(b["sb"].at[self.slot(u), :, :, 0:MAIN], self.far_land.at[self.mats(u), :, 0:MAIN]),
                          (b["st"].at[self.slot(u)], self.far_tail.at[u])]
             return [remote(src, dst, b["rs_s"].at[u, i], b["rs_r"].at[u, i], far_same) for i, (src, dst) in enumerate(pairs)]
 
@@ -330,7 +336,7 @@
             for index, chunk in enumerate(kind.chunks):
                 mat, nmat, row, nrow = chunk
                 if kind.tail:
-                    far_copies = [local(self.far_land.at[self.mats(u), :, 0:384], b["xl"].at[:, :, 0:384], b["loc"].at[6]),
+                    far_copies = [local(self.far_land.at[self.mats(u), :, 0:MAIN], b["xl"].at[:, :, 0:MAIN], b["loc"].at[6]),
                                   local(self.far_tail.at[u], b["xt"], b["loc"].at[10])]
                 else:
                     far_copies = [local(self.far_land.at[self.mats(u, mat, nmat), pl.ds(row, nrow), :], b["xl"], b["loc"].at[6])]
@@ -346,9 +352,9 @@
                     copy.wait()
                 for i in range(nmat):
                     if kind.tail:
-                        lane = i // kind.pair * 64
-                        cuts = ((slice(0, 384), b["xl"][i, :, 0:384]),
-                                (slice(384, 448), b["xt"][i % kind.pair][:, lane:lane + 64]))
+                        lane = i // kind.pair * TAIL
+                        cuts = ((slice(0, MAIN), b["xl"][i, :, 0:MAIN]),
+                                (slice(MAIN, MAIN + TAIL), b["xt"][i % kind.pair][:, lane:lane + TAIL]))
                     else:
                         cuts = ((slice(0, kind.q_cols), b["xl"][i]),)
                     for cut, far_sum in cuts:
@@ -358,7 +364,7 @@
                         sq_sum = jnp.sum(jnp.sum(value * value, axis=0, keepdims=True), axis=1, keepdims=True)
                         sums[mat + i] = sq_sum if sums[mat + i] is None else sums[mat + i] + sq_sum
             for i in range(kind.unit):
-                b["nr"][u, me, i:i + 1, :] = jnp.broadcast_to(sums[i], (1, 128))
+                b["nr"][u, me, i:i + 1, :] = jnp.broadcast_to(sums[i], (1, LANE))
             self.mom_out(u).start()
 
         def norm_start(self, u):
@@ -376,9 +382,9 @@
             else:
                 routes = [(b["xs"].at[slot], place, partner), (b["xs"].at[slot], place, far_same)]
             if kind.half_pair:
-                main = b["xg"].at[u, :, block_of(kind, me)[0], 0:384]
+                main = b["xg"].at[u, :, block_of(kind, me)[0], 0:MAIN]
                 for h, base in enumerate((core * kind.half, other * kind.half)):
-                    routes[1 + h] = (b["xs"].at[slot, pl.ds(base, kind.half), :, 0:384], main, routes[1 + h][2])
+                    routes[1 + h] = (b["xs"].at[slot, pl.ds(base, kind.half), :, 0:MAIN], main, routes[1 + h][2])
                 routes += [(b["xts"].at[slot, h], b["xtq"].at[u, h], device) for h, device in enumerate((far_same, far_other))]
             return [remote(src, dst, b["x_s"].at[u, i], b["x_r"].at[u, i], device) for i, (src, dst, device) in enumerate(routes)]
 
@@ -429,8 +435,8 @@
                     for i in range(kind.half_pair):
                         both = b["xtq"][u, h, i].astype(F32)
                         for side in range(2):
-                            part = both[:, 64 * side:64 * side + 64].astype(BF16)
-                            b["xg"][u, i + side * kind.half_pair, block_of(kind, device)[0], 384:448] = part
+                            part = both[:, TAIL * side:TAIL * side + TAIL].astype(BF16)
+                            b["xg"][u, i + side * kind.half_pair, block_of(kind, device)[0], MAIN:MAIN + TAIL] = part
             newton_schulz(self.kind, self.b["xg"], u, gram_acc)
 
         def iterate_start(self, u):
@@ -442,18 +448,18 @@
 
         def param_out(self, u):
             if self.kind.late:
-                return local(self.rounded(), self.param.at[self.mats(u)], self.b["loc"].at[9])
-            return local(self.rounded(), self.param.at[(self.mats(u),) + block_of(self.kind, me)], self.b["loc"].at[9])
+                return local(self.rounded(u), self.param.at[self.mats(u)], self.b["loc"].at[14 + self.slot(u)])
+            return local(self.rounded(u), self.param.at[(self.mats(u),) + block_of(self.kind, me)], self.b["loc"].at[14 + self.slot(u)])
 
         def param_sends(self, u):
             kind, b = self.kind, self.b
             if kind.late:
                 return []
             place = self.param.at[(self.mats(u),) + block_of(kind, me)]
-            routes = [(self.rounded(), place, partner, 0), (self.rounded(), place, far_same, 1)]
+            routes = [(self.rounded(u), place, partner, 0), (self.rounded(u), place, far_same, 1)]
             if kind.tail:
-                main = self.param.at[self.mats(u), block_of(kind, me)[0], 0:384]
-                routes[1:] = [(b["pb"].at[:, :, 0:384], main, far_same, 1), (b["pst"], b["ptq"].at[u], far_same, 3)]
+                main = self.param.at[self.mats(u), block_of(kind, me)[0], 0:MAIN]
+                routes[1:] = [(b["pb"].at[self.slot(u), :, :, 0:MAIN], main, far_same, 1), (b["pst"].at[self.slot(u)], b["ptq"].at[u], far_same, 3)]
             return [remote(src, dst, b["p_s"].at[u, i], b["p_r"].at[u, i], device) for src, dst, device, i in routes]
 
         def param_forwards(self, u):
@@ -463,12 +469,12 @@
             place = self.param.at[(self.mats(u),) + block_of(kind, far_same)]
             routes = [(place, place, 2)]
             if kind.tail:
-                main = self.param.at[self.mats(u), block_of(kind, far_same)[0], 0:384]
+                main = self.param.at[self.mats(u), block_of(kind, far_same)[0], 0:MAIN]
                 routes = [(main, main, 2), (b["ptu"], self.tail_place(u), 4)]
             return [remote(src, dst, b["p_s"].at[u, i], b["p_r"].at[u, i], partner) for src, dst, i in routes]
 
         def tail_place(self, u):
-            return self.param.at[self.mats(u), block_of(self.kind, far_same)[0], 384:448]
+            return self.param.at[self.mats(u), block_of(self.kind, far_same)[0], MAIN:MAIN + TAIL]
 
         def tail_out(self, u):
             return local(self.b["ptu"], self.tail_place(u), self.b["loc"].at[11])
@@ -488,10 +494,11 @@
                     old = weight[base + j]
                     new = old - LEARN_RATE * (kind.scale * ortho(j).astype(F32) + WEIGHT_DECAY * old)
                     weight[base + j] = new
-                    self.rounded()[base + j] = new.astype(BF16)
-            if kind.tail:
+                    self.rounded(u)[base + j] = new.astype(BF16)
+            if kind.tail and not kind.late:
                 for i in range(kind.pair):
-                    b["pst"][i] = join(b["pb"][i].astype(F32), b["pb"][i + kind.pair].astype(F32)).astype(BF16)
+                    left, right = (b["pb"][self.slot(u), j].astype(F32) for j in (i, i + kind.pair))
+                    b["pst"][self.slot(u), i] = join(left, right).astype(BF16)
 
         def update_start(self, u):
             self.weight_out(u).start()
@@ -507,16 +514,16 @@
             for copy in self.param_sends(u):
                 copy.wait()
             kind, b = self.kind, self.b
-            if kind.tail:
+            if kind.tail and not kind.late:
                 for i in range(kind.unit):
-                    lane = i // kind.pair * 64
-                    b["ptu"][i] = b["ptq"][u, i % kind.pair].astype(F32)[:, lane:lane + 64].astype(BF16)
+                    lane = i // kind.pair * TAIL
+                    b["ptu"][i] = b["ptq"][u, i % kind.pair].astype(F32)[:, lane:lane + TAIL].astype(BF16)
                 self.tail_out(u).start()
             for copy in self.param_forwards(u):
                 copy.start()
 
         def finish(self, u):
-            if self.kind.tail:
+            if self.kind.tail and not self.kind.late:
                 self.tail_out(u).wait()
             for copy in self.param_forwards(u):
                 copy.wait()
@@ -552,7 +559,7 @@
 
             def far_piece(i, j, r):
                 both = b["gf"][i, r * cut:(r + 1) * cut, :] + b["df"][i, r * cut:(r + 1) * cut, :]
-                quarters = [both[:, 112 * d:112 * (d + 1)] for d in range(4)]
+                quarters = [both[:, BLOCK * d:BLOCK * (d + 1)] for d in range(4)]
                 if j == 0:
                     near = [jnp.where(chip == 0, quarters[d], quarters[2 + d]) for d in range(2)]
                     b["nb"][slot, 0, i, r * cut:(r + 1) * cut, :] = jnp.where(core == 0, near[0], near[1])
@@ -583,11 +590,11 @@
             for i in range(kind.half):
                 for r in range(2):
                     rows = slice(r * cut, (r + 1) * cut)
-                    first = b["xl"][i * 4 + r][:, :112]
+                    first = b["xl"][i * 4 + r][:, :BLOCK]
                     if i * 4 + 2 + r < 7:
-                        second = b["xl"][i * 4 + 2 + r][:, :112]
+                        second = b["xl"][i * 4 + 2 + r][:, :BLOCK]
                     else:
-                        second = jnp.concatenate([b["xl"][g][:, 112:128] for g in range(7)], axis=1)
+                        second = jnp.concatenate([b["xl"][g][:, BLOCK:LANE] for g in range(7)], axis=1)
                     b["nb"][slot, 0, i, rows, :] = b["nb"][slot, 0, i, rows, :] + jnp.where(core == 0, first, second)
                     b["tq"][i, rows, :] = b["nb"][slot, 1, i, rows, :] + jnp.where(core == 0, second, first)
 
@@ -608,11 +615,11 @@
                     value = MOMENTUM * b["mo"][slot, base + i] + total(i) * 0.25
                     b["mo"][slot, base + i] = value
                     sq_sum = jnp.sum(jnp.sum(value * value, axis=0, keepdims=True), axis=1, keepdims=True)
-                    b["nr"][u, me, pl.ds(base + i, 1), :] = jnp.broadcast_to(sq_sum, (1, 128))
+                    b["nr"][u, me, pl.ds(base + i, 1), :] = jnp.broadcast_to(sq_sum, (1, LANE))
             self.mom_out(u).start()
 
         def lane_block(self, device):
-            return pl.ds(pl.multiple_of(device * 128, 128), 128)
+            return pl.ds(pl.multiple_of(device * LANE, LANE), LANE)
 
         def start_sends(self, u):
             kind, b = self.kind, self.b
@@ -638,7 +645,7 @@
             b["xg"][u, :, :, self.lane_block(me)] = b["xs"][slot, pl.ds(core * kind.half, kind.half)]
             cut = kind.rows // 4
             for h, base in enumerate((core * kind.half, other * kind.half)):
-                pieces = [b["xs"][slot, base + g // 4, g % 4 * cut:(g % 4 + 1) * cut, :].astype(F32)[:, :112] for g in range(8)]
+                pieces = [b["xs"][slot, base + g // 4, g % 4 * cut:(g % 4 + 1) * cut, :].astype(F32)[:, :BLOCK] for g in range(8)]
                 for g, block in enumerate(pack(pieces)):
                     b["xp"][slot, h, g] = block.astype(BF16)
             self.mom_out(u).wait()
@@ -661,13 +668,13 @@
             return remote(b["xg"].at[u, :, :, self.lane_block(partner)], b["orow"].at[u], b["o_s"].at[u, 0], b["o_r"].at[u, 0], partner)
 
         def param_out(self, u):
-            return local(self.b["pk"], self.param_land.at[u, me], self.b["loc"].at[9])
+            return local(self.b["pk"].at[self.slot(u)], self.param_land.at[u, me], self.b["loc"].at[14 + self.slot(u)])
 
         def param_sends(self, u):
             b = self.b
             place = self.param_land.at[u, me]
             return [
-                remote(b["pk"], place, b["p_s"].at[u, i], b["p_r"].at[u, i], device)
+                remote(b["pk"].at[self.slot(u)], place, b["p_s"].at[u, i], b["p_r"].at[u, i], device)
                 for i, device in enumerate((partner, far_same))
             ]
 
@@ -686,13 +693,13 @@
             for base, ortho in parts:
                 for j in range(kind.half):
                     old = weight[base + j]
-                    new = old - LEARN_RATE * (kind.scale * ortho(j).astype(F32)[:, :112] + WEIGHT_DECAY * old)
+                    new = old - LEARN_RATE * (kind.scale * ortho(j).astype(F32)[:, :BLOCK] + WEIGHT_DECAY * old)
                     weight[base + j] = new
                     b["pb"][base + j] = new.astype(BF16)
             cut = kind.rows // 2
             pieces = [b["pb"][g // 2, g % 2 * cut:(g % 2 + 1) * cut, :].astype(F32) for g in range(8)]
             for g, block in enumerate(pack(pieces)):
-                b["pk"][g] = block.astype(BF16)
+                b["pk"][self.slot(u), g] = block.astype(BF16)
 
         def matrix_out(self, u):
             return local(self.b["pa"], self.param.at[self.mats(u)], self.b["loc"].at[2])
@@ -707,7 +714,7 @@
             cut = kind.rows // 2
             for g in range(8):
                 if g < 7:
-                    quarters = [b["pv"][d, g].astype(F32)[:, :112] for d in range(4)]
+                    quarters = [b["pv"][d, g].astype(F32)[:, :BLOCK] for d in range(4)]
                 else:
                     quarters = [unpack([b["pv"][d, k].astype(F32) for k in range(7)])[7] for d in range(4)]
                 b["pa"][g // 2, g % 2 * cut:(g % 2 + 1) * cut, :] = jnp.concatenate(quarters, axis=1).astype(BF16)
@@ -722,16 +729,6 @@
     for k in ORDER:
         bases[k] = total_units
         total_units += kinds[k].units
-
-    for k in ORDER:
-        stage = stages[k]
-
-        def send_all(u, carry, stage=stage):
-            for copy in stage.exchange(u):
-                copy.start()
-            return carry
-
-        lax.fori_loop(0, kinds[k].units, send_all, 0)
 
     def step(t, carry):
         def run(name, lag):
@@ -746,10 +743,10 @@
                     method(u)
 
         for name, lag in SCHEDULE:
-            run(name, LAGS[lag])
+            run(name, lag)
         return carry
 
-    lax.fori_loop(0, total_units + LAGS[-1], step, 0)
+    lax.fori_loop(0, total_units + STEPS_BEHIND, step, 0)
 
 
 def copy_kernel(cuts, num, *refs):
@@ -786,39 +783,50 @@
     )(*arrays)
 
 
-def gather_kernel(own, far, near, near_far, target, *rest):
-    stores, sem = rest[:4], rest[4]
+def gather_kernel(num, *refs):
+    sources, targets, stores, sems = refs[:4 * num], refs[4 * num:5 * num], refs[5 * num:8 * num], refs[8 * num:]
     me = lax.axis_index("data")
     chip, core = me // 2, me % 2
     places = (me, 2 * (1 - chip) + core, 2 * chip + 1 - core, 2 * (1 - chip) + 1 - core)
-    rows = own.shape[1]
-    loads = [pltpu.make_async_copy(source, stores[i], sem.at[0, i]) for i, source in enumerate((own, far, near, near_far))]
-    saves = [pltpu.make_async_copy(stores[i], target.at[:, pl.ds(pl.multiple_of(place * rows, 16), rows), :], sem.at[1, i])
-             for i, place in enumerate(places)]
+    loads, saves = [], []
+    for k in range(num):
+        rows = sources[k].shape[1]
+        for i, place in enumerate(places):
+            source = sources[i * num + k]
+            if i < 3:
+                store = stores[i * num + k]
+                loads.append(pltpu.make_async_copy(source, store, sems[0].at[i, k]))
+                source = store
+            cut = pl.ds(pl.multiple_of(place * rows, PAD), rows)
+            saves.append((i < 3, pltpu.make_async_copy(source, targets[k].at[:, cut, :], sems[1].at[i, k])))
     for load in loads:
         load.start()
-    for load, save in zip(loads, saves):
-        load.wait()
-        save.start()
-    for save in saves:
+    for ready in (False, True):
+        for load in loads if ready else []:
+            load.wait()
+        for waits, save in saves:
+            if waits == ready:
+                save.start()
+    for _, save in saves:
         save.wait()
 
 
-def gather_rows(own, arrays):
-    far = lax.ppermute(own, "data", [(0, 2), (2, 0), (1, 3), (3, 1)])
+def gather_rows(owns, arrays):
+    num = len(owns)
     cores = [(0, 1), (1, 0), (2, 3), (3, 2)]
-    near = lax.ppermute(own, "data", cores)
+    fars = [lax.ppermute(own, "data", [(0, 2), (2, 0), (1, 3), (3, 1)]) for own in owns]
+    nears = [lax.ppermute(own, "data", cores) for own in owns]
     copied = copy_out(arrays, 4)
-    far, near, copied = lax.optimization_barrier((far, near, copied))
-    near_far = lax.ppermute(far, "data", cores)
+    fars, nears, copied = lax.optimization_barrier((fars, nears, copied))
+    near_fars = [lax.ppermute(far, "data", cores) for far in fars]
     gathered = pl.pallas_call(
-        gather_kernel,
-        out_shape=jax.ShapeDtypeStruct((own.shape[0], 4 * own.shape[1], own.shape[2]), own.dtype),
-        in_specs=[pl.BlockSpec(memory_space=pl.ANY)] * 4,
-        out_specs=pl.BlockSpec(memory_space=pl.ANY),
-        scratch_shapes=[pltpu.VMEM(own.shape, own.dtype)] * 4 + [pltpu.SemaphoreType.DMA((2, 4))],
-        cost_estimate=pl.CostEstimate(flops=0, bytes_accessed=8 * own.size * 2, transcendentals=0),
-    )(own, far, near, near_far)
+        functools.partial(gather_kernel, num),
+        out_shape=[jax.ShapeDtypeStruct((own.shape[0], 4 * own.shape[1], own.shape[2]), own.dtype) for own in owns],
+        in_specs=[pl.BlockSpec(memory_space=pl.ANY)] * (3 * num) + [pl.BlockSpec(memory_space=pltpu.VMEM)] * num,
+        out_specs=[pl.BlockSpec(memory_space=pl.ANY)] * num,
+        scratch_shapes=[pltpu.VMEM(own.shape, own.dtype) for own in owns] * 3 + [pltpu.SemaphoreType.DMA((4, num))] * 2,
+        cost_estimate=pl.CostEstimate(flops=0, bytes_accessed=16 * sum(own.size for own in owns), transcendentals=0),
+    )(*owns, *fars, *nears, *near_fars)
     return gathered, copied
 
 
@@ -839,9 +847,9 @@
         far_shapes = list(row_shapes)
         lane = kinds[3]
         land_shapes[3] = jax.ShapeDtypeStruct((lane.count // 2, lane.rows, lane.cols), F32)
-        far_shapes[3] = jax.ShapeDtypeStruct((lane.units, 7, lane.rows // 2, 128), F32)
-        param_shape = jax.ShapeDtypeStruct((lane.units, 4, 7, lane.rows // 2, 128), BF16)
-        tail_shapes = [jax.ShapeDtypeStruct((kind.units, kind.pair, kind.q_rows, 128), F32) for kind in kinds if kind.tail]
+        far_shapes[3] = jax.ShapeDtypeStruct((lane.units, 7, lane.rows // 2, LANE), F32)
+        param_shape = jax.ShapeDtypeStruct((lane.units, 4, 7, lane.rows // 2, LANE), BF16)
+        tail_shapes = [jax.ShapeDtypeStruct((kind.units, kind.pair, kind.q_rows, LANE), F32) for kind in kinds if kind.tail]
         flipped = [jnp.swapaxes(array, -1, -2) if kinds[i % num].flip else array for i, array in enumerate(arrays)]
         outs = pl.pallas_call(
             functools.partial(kernel, kinds, names),
@@ -854,10 +862,10 @@
             ),
         )(*flipped)
         outs = list(outs[:3 * num])
-        late = next(2 * num + kind.index for kind in kinds if kind.late)
-        early = [i for i in range(3 * num) if i != late]
-        gathered, copied = gather_rows(outs[late], [outs[i] for i in early])
-        for i, array in zip(early + [late], list(copied) + [gathered]):
+        late = [2 * num + kind.index for kind in kinds if kind.late]
+        early = [i for i in range(3 * num) if i not in late]
+        gathered, copied = gather_rows([outs[i] for i in late], [outs[i] for i in early])
+        for i, array in zip(early + late, list(copied) + list(gathered)):
             outs[i] = array
         return tuple(jnp.swapaxes(array, -1, -2) if kinds[i % num].flip else array for i, array in enumerate(outs[:3 * num]))
 

time: 527 us -> 523 us (level)
    pallas_call x1, Pallas kernels: 486 us -> 480 us  [local_step(): pl.pallas_call(functools.partial(kernel, kinds, names), out_shape=row_sha...]
where the time goes in v5:
time: 523 us; the launch traced here: 522 us
  Pallas kernels  516 us (99%)
    pallas_call x1, Pallas kernels, local_step(): pl.pallas_call(functools.partial(kernel, kinds, names), out_shape=row_sha...  480 us
    pallas_call x1, Pallas kernels, copy_out(): pl.pallas_call(functools.partial(copy_kernel, cuts, len(arrays)), out_sha...  30.6 us
  transfers between devices with their start and end apart: 3, of which 1 were waited for; matrix products, arithmetic and copies ran while one was open for 0% of the time, Pallas kernels for 6%

profile of v5, /device:TPU:0, one launch (start us, length us, event | category | flops | bytes accessed | tf_op | source)
XLA Modules:
  0.0 521.9 jit_solution(13280201002487677673)
XLA Ops:
  0.7 479.7 %shard_map.262 = (f32[4,112,448]{2,1,0:T(8,128)}, f32[2,112,2560]{2,1,0:T(8,128)}, f32[1,448,640]{2,1,0:T(8,128)}, f32[32,320,112]{2,1,0:T(8,128)}, f32[16,80,44...) custom-call(f32[1,4,448,448]{3,2,1,0:T(8,128)} %refs_0_.1, ...), custom_call_target="tpu_custom_call" | custom-call | tf_op jit(solution)/shard_map/pallas_call | solution.py:854
  480.4 0.0 collective-permute-start.1
  480.4 1.5 collective-permute-start
  481.9 30.6 %shard_map.263 = (f32[4,112,448]{2,1,0:T(8,128)}, f32[2,112,2560]{2,1,0:T(8,128)}, f32[1,448,640]{2,1,0:T(8,128)}, f32[32,320,112]{2,1,0:T(8,128)}, f32[16,80,44...) custom-call(f32[4,112,448]{2,1,0:T(8,128)} %get-tuple-element.61.ref, ...), custom_call_target="tpu_custom_call" | custom-call | flops 47893708800 | bytes 79822848 | tf_op jit(solution)/shard_map/pallas_call | solution.py:774
  512.5 0.0 collective-permute-done.1.refs_2_
  512.5 0.0 collective-permute-done.refs_1_
  512.5 0.2 collective-permute-start.2
  512.7 2.6 collective-permute-done.2.refs_3_
  515.3 0.0 copy-start
  515.3 1.0 copy-done
  516.3 5.4 %shard_map.264 = bf16[2,448,2560]{2,1,0:T(8,128)(2,1)} custom-call(bf16[2,112,2560]{2,1,0:T(8,128)(2,1)} %get-tuple-element.60.refs_0_, bf16[2,112,2560]{2,1,0:T(8,128)(2,1)} %collective-permute-done.refs_1_, bf16[2,112,2560]{2,1,0:T(8,128)(2,1)} %collective-permute-done.1.refs_2_, bf16[2,112,2560]{2,1,0:T(8,128)(2,1)} %copy-done), custom_call_target="tpu_custom_call" | custom-call | bytes 9175040 | tf_op jit(solution)/shard_map/pallas_call | solution.py:822
Async XLA Ops:
  480.4 32.1 %collective-permute-start.1 = (bf16[2,112,2560]{2,1,0:T(8,128)(2,1)}, bf16[2,112,2560]{2,1,0:T(8,128)(2,1)}, u32[]{:S(2)}, u32[]{:S(2)}) collective-permute-start(bf16[2,112,2560]{2,1,0:T(8,128)(2,1)} %get-tuple-element.60.refs_0_), channel_id=1, source_target_pairs={{0,1},{1,0},{2,3},{3,2},{4,5},{5,4},{6,7},{7,6}} | collective-permute-start | bytes 3440648 | tf_op jit(solution)/shard_map/ppermute | solution.py:818
  480.4 32.1 %collective-permute-start = (bf16[2,112,2560]{2,1,0:T(8,128)(2,1)}, bf16[2,112,2560]{2,1,0:T(8,128)(2,1)}, u32[]{:S(2)}, u32[]{:S(2)}) collective-permute-start(bf16[2,112,2560]{2,1,0:T(8,128)(2,1)} %get-tuple-element.60.refs_0_), channel_id=1, source_target_pairs={{0,2},{2,0},{1,3},{3,1},{4,6},{6,4},{5,7},{7,5}} | collective-permute-start | bytes 3440648 | tf_op jit(solution)/shard_map/ppermute | solution.py:817
  512.5 2.8 collective-permute-start.2
  515.3 1.0 copy-start

commit v6 on v5

--- a/solution.py
+++ b/solution.py
@@ -749,13 +749,27 @@
     lax.fori_loop(0, total_units + STEPS_BEHIND, step, 0)
 
 
-def copy_kernel(cuts, num, *refs):
-    sources, targets, stores = refs[:num], refs[num:2 * num], refs[2 * num:3 * num]
-    in_sem, out_sem = refs[3 * num:]
-    loads = [pltpu.make_async_copy(sources[i].at[pl.ds(lo, size)], stores[i].at[pl.ds(lo, size)], in_sem.at[n])
-             for n, (i, lo, size) in enumerate(cuts)]
-    saves = [pltpu.make_async_copy(stores[i].at[pl.ds(lo, size)], targets[i].at[pl.ds(lo, size)], out_sem.at[n])
-             for n, (i, lo, size) in enumerate(cuts)]
+def row_cut(array, place):
+    rows = array.shape[1]
+    return pl.ds(pl.multiple_of(place * rows, PAD), rows)
+
+
+def copy_kernel(cuts, num, parts, *refs):
+    total = num + parts
+    sources, refs = refs[:total], refs[total:]
+    targets, refs = refs[:num], refs[num:]
+    if parts:
+        whole, refs = refs[0], refs[1:]
+    stores, (in_sem, out_sem) = refs[:total], refs[total:]
+    routes = [(sources[i].at[pl.ds(lo, size)], stores[i].at[pl.ds(lo, size)], targets[i].at[pl.ds(lo, size)]) for i, lo, size in cuts]
+    if parts:
+        me = lax.axis_index("data")
+        chip, core = me // 2, me % 2
+        places = (me, 2 * (1 - chip) + core, 2 * chip + 1 - core)
+        routes += [(source, store, whole.at[:, row_cut(source, place), :])
+                   for source, store, place in zip(sources[num:], stores[num:], places)]
+    loads = [pltpu.make_async_copy(source, store, in_sem.at[n]) for n, (source, store, _) in enumerate(routes)]
+    saves = [pltpu.make_async_copy(store, target, out_sem.at[n]) for n, (_, store, target) in enumerate(routes)]
     for load in loads:
         load.start()
     for load, save in zip(loads, saves):
@@ -765,69 +779,57 @@
         save.wait()
 
 
-def copy_out(arrays, pieces):
+def copy_out(arrays, pieces, parts=()):
     cuts = []
     for i, array in enumerate(arrays):
         size = max(1, array.shape[0] // pieces)
         cuts += [(i, lo, size) for lo in range(0, array.shape[0], size)]
     total = sum(array.size * array.dtype.itemsize for array in arrays)
+    shapes = [jax.ShapeDtypeStruct(array.shape, array.dtype) for array in arrays]
+    if parts:
+        count, rows, cols = parts[0].shape
+        shapes.append(jax.ShapeDtypeStruct((count, 4 * rows, cols), parts[0].dtype))
     return pl.pallas_call(
-        functools.partial(copy_kernel, cuts, len(arrays)),
-        out_shape=[jax.ShapeDtypeStruct(array.shape, array.dtype) for array in arrays],
-        in_specs=[pl.BlockSpec(memory_space=pl.ANY)] * len(arrays),
-        out_specs=[pl.BlockSpec(memory_space=pl.ANY)] * len(arrays),
-        scratch_shapes=[pltpu.VMEM(array.shape, array.dtype) for array in arrays]
-        + [pltpu.SemaphoreType.DMA((len(cuts),))] * 2,
+        functools.partial(copy_kernel, cuts, len(arrays), len(parts)),
+        out_shape=shapes,
+        in_specs=[pl.BlockSpec(memory_space=pl.ANY)] * (len(arrays) + len(parts)),
+        out_specs=[pl.BlockSpec(memory_space=pl.ANY)] * len(shapes),
+        scratch_shapes=[pltpu.VMEM(array.shape, array.dtype) for array in (*arrays, *parts)]
+        + [pltpu.SemaphoreType.DMA((len(cuts) + len(parts),))] * 2,
         compiler_params=pltpu.CompilerParams(vmem_limit_bytes=67043328),
         cost_estimate=pl.CostEstimate(flops=1200 * total, bytes_accessed=2 * total, transcendentals=0),
-    )(*arrays)
-
-
-def gather_kernel(num, *refs):
-    sources, targets, stores, sems = refs[:4 * num], refs[4 * num:5 * num], refs[5 * num:8 * num], refs[8 * num:]
+    )(*arrays, *parts)
+
+
+def place_kernel(rows, _, whole, store, sem):
     me = lax.axis_index("data")
-    chip, core = me // 2, me % 2
-    places = (me, 2 * (1 - chip) + core, 2 * chip + 1 - core, 2 * (1 - chip) + 1 - core)
-    loads, saves = [], []
-    for k in range(num):
-        rows = sources[k].shape[1]
-        for i, place in enumerate(places):
-            source = sources[i * num + k]
-            if i < 3:
-                store = stores[i * num + k]
-                loads.append(pltpu.make_async_copy(source, store, sems[0].at[i, k]))
-                source = store
-            cut = pl.ds(pl.multiple_of(place * rows, PAD), rows)
-            saves.append((i < 3, pltpu.make_async_copy(source, targets[k].at[:, cut, :], sems[1].at[i, k])))
-    for load in loads:
-        load.start()
-    for ready in (False, True):
-        for load in loads if ready else []:
-            load.wait()
-        for waits, save in saves:
-            if waits == ready:
-                save.start()
-    for _, save in saves:
-        save.wait()
-
-
-def gather_rows(owns, arrays):
-    num = len(owns)
+    place = 2 * (1 - me // 2) + 1 - me % 2
+    load = pltpu.make_async_copy(rows, store, sem.at[0])
+    save = pltpu.make_async_copy(store, whole.at[:, row_cut(rows, place), :], sem.at[1])
+    load.start()
+    load.wait()
+    save.start()
+    save.wait()
+
+
+def gather_rows(own, arrays, later):
     cores = [(0, 1), (1, 0), (2, 3), (3, 2)]
-    fars = [lax.ppermute(own, "data", [(0, 2), (2, 0), (1, 3), (3, 1)]) for own in owns]
-    nears = [lax.ppermute(own, "data", cores) for own in owns]
+    far = lax.ppermute(own, "data", [(0, 2), (2, 0), (1, 3), (3, 1)])
+    near = lax.ppermute(own, "data", cores)
     copied = copy_out(arrays, 4)
-    fars, nears, copied = lax.optimization_barrier((fars, nears, copied))
-    near_fars = [lax.ppermute(far, "data", cores) for far in fars]
-    gathered = pl.pallas_call(
-        functools.partial(gather_kernel, num),
-        out_shape=[jax.ShapeDtypeStruct((own.shape[0], 4 * own.shape[1], own.shape[2]), own.dtype) for own in owns],
-        in_specs=[pl.BlockSpec(memory_space=pl.ANY)] * (3 * num) + [pl.BlockSpec(memory_space=pltpu.VMEM)] * num,
-        out_specs=[pl.BlockSpec(memory_space=pl.ANY)] * num,
-        scratch_shapes=[pltpu.VMEM(own.shape, own.dtype) for own in owns] * 3 + [pltpu.SemaphoreType.DMA((4, num))] * 2,
-        cost_estimate=pl.CostEstimate(flops=0, bytes_accessed=16 * sum(own.size for own in owns), transcendentals=0),
-    )(*owns, *fars, *nears, *near_fars)
-    return gathered, copied
+    far, near, later, copied = lax.optimization_barrier((far, near, later, copied))
+    near_far = lax.ppermute(far, "data", cores)
+    *copied_later, whole = copy_out(later, 4, (own, far, near))
+    near_far, whole = lax.optimization_barrier((near_far, whole))
+    whole = pl.pallas_call(
+        place_kernel,
+        out_shape=jax.ShapeDtypeStruct(whole.shape, whole.dtype),
+        in_specs=[pl.BlockSpec(memory_space=pl.ANY)] * 2,
+        out_specs=pl.BlockSpec(memory_space=pl.ANY),
+        scratch_shapes=[pltpu.VMEM(own.shape, own.dtype), pltpu.SemaphoreType.DMA((2,))],
+        input_output_aliases={1: 0},
+    )(near_far, whole)
+    return list(copied) + copied_later + [whole]
 
 
 def solution(mesh):
@@ -862,10 +864,11 @@
             ),
         )(*flipped)
         outs = list(outs[:3 * num])
-        late = [2 * num + kind.index for kind in kinds if kind.late]
-        early = [i for i in range(3 * num) if i not in late]
-        gathered, copied = gather_rows([outs[i] for i in late], [outs[i] for i in early])
-        for i, array in zip(early + late, list(copied) + list(gathered)):
+        late = next(2 * num + kind.index for kind in kinds if kind.late)
+        later = [1, num - 1]
+        early = [i for i in range(3 * num) if i != late and i not in later]
+        finals = gather_rows(outs[late], [outs[i] for i in early], [outs[i] for i in later])
+        for i, array in zip(early + later + [late], finals):
             outs[i] = array
         return tuple(jnp.swapaxes(array, -1, -2) if kinds[i % num].flip else array for i, array in enumerate(outs[:3 * num]))
 

time: 523 us -> 520 us (level)
    pallas_call x2 -> x3, Pallas kernels: 36 us -> 35.9 us  [the longest x2 33.6 us: copy_out(): pl.pallas_call(functools.partial(copy_kernel, cuts, len(arrays), len(part...]
  transfers between devices with their start and end apart: 3 -> 3, of which waited for: 1 -> 0; matrix products, arithmetic and copies ran while one was open for 0% -> 0% of each run, Pallas kernels for 6% -> 6%
where the time goes in v6:
time: 520 us; the launch traced here: 518 us
  Pallas kernels  516 us (99%)
    pallas_call x1, Pallas kernels, local_step(): pl.pallas_call(functools.partial(kernel, kinds, names), out_shape=row_sha...  480 us
    pallas_call x2, Pallas kernels, copy_out(): pl.pallas_call(functools.partial(copy_kernel, cuts, len(arrays), len(part...  33.6 us
  transfers between devices with their start and end apart: 3, of which 0 were waited for; matrix products, arithmetic and copies ran while one was open for 0% of the time, Pallas kernels for 6%

profile of v6, /device:TPU:0, one launch (start us, length us, event | category | flops | bytes accessed | tf_op | source)
XLA Modules:
  0.0 518.2 jit_solution(1262769542666811846)
XLA Ops:
  0.7 479.7 %shard_map.262 = (f32[4,112,448]{2,1,0:T(8,128)}, f32[2,112,2560]{2,1,0:T(8,128)}, f32[1,448,640]{2,1,0:T(8,128)}, f32[32,320,112]{2,1,0:T(8,128)}, f32[16,80,44...) custom-call(f32[1,4,448,448]{3,2,1,0:T(8,128)} %refs_0_.1, ...), custom_call_target="tpu_custom_call" | custom-call | tf_op jit(solution)/shard_map/pallas_call | solution.py:856
  480.4 0.0 collective-permute-start.1
  480.4 1.5 collective-permute-start
  481.9 27.0 %shard_map.263 = (f32[4,112,448]{2,1,0:T(8,128)}, f32[1,448,640]{2,1,0:T(8,128)}, f32[32,320,112]{2,1,0:T(8,128)}, f32[4,112,448]{2,1,0:T(8,128)}, f32[2,112,256...) custom-call(f32[4,112,448]{2,1,0:T(8,128)} %get-tuple-element.66.ref, ...), custom_call_target="tpu_custom_call" | custom-call | flops 42388684800 | bytes 70647808 | tf_op jit(solution)/shard_map/pallas_call | solution.py:792
  508.9 0.0 collective-permute-done.1.refs_4_
  508.9 0.0 collective-permute-done.refs_3_
  508.9 0.2 collective-permute-start.2
  509.1 6.6 %shard_map.264 = (f32[2,112,2560]{2,1,0:T(8,128)}, f32[16,80,448]{2,1,0:T(8,128)}, bf16[2,448,2560]{2,1,0:T(8,128)(2,1)}) custom-call(f32[2,112,2560]{2,1,0:T(8,128)} %get-tuple-element.91.refs_0_, f32[16,80,448]{2,1,0:T(8,128)} %get-tuple-element.92.refs_1_, bf16[2,112,2560]{2,1,0:T(8,128)(2,1)} %get-tuple-element.63.refs_2_, ...), custom_call_target="tpu_custom_call" | custom-call | flops 5505024000 | bytes 9175040 | tf_op jit(solution)/shard_map/pallas_call | solution.py:792
  515.8 0.0 collective-permute-done.2.rows
  515.8 2.3 shard_map.265
Async XLA Ops:
  480.4 28.5 %collective-permute-start.1 = (bf16[2,112,2560]{2,1,0:T(8,128)(2,1)}, bf16[2,112,2560]{2,1,0:T(8,128)(2,1)}, u32[]{:S(2)}, u32[]{:S(2)}) collective-permute-start(bf16[2,112,2560]{2,1,0:T(8,128)(2,1)} %get-tuple-element.63.refs_2_), channel_id=1, source_target_pairs={{0,1},{1,0},{2,3},{3,2},{4,5},{5,4},{6,7},{7,6}} | collective-permute-start | bytes 3440648 | tf_op jit(solution)/shard_map/ppermute | solution.py:818
  480.4 28.5 %collective-permute-start = (bf16[2,112,2560]{2,1,0:T(8,128)(2,1)}, bf16[2,112,2560]{2,1,0:T(8,128)(2,1)}, u32[]{:S(2)}, u32[]{:S(2)}) collective-permute-start(bf16[2,112,2560]{2,1,0:T(8,128)(2,1)} %get-tuple-element.63.refs_2_), channel_id=1, source_target_pairs={{0,2},{2,0},{1,3},{3,1},{4,6},{6,4},{5,7},{7,5}} | collective-permute-start | bytes 3440648 | tf_op jit(solution)/shard_map/ppermute | solution.py:817
  508.9 6.9 %collective-permute-start.2 = (bf16[2,112,2560]{2,1,0:T(8,128)(2,1)}, bf16[2,112,2560]{2,1,0:T(8,128)(2,1)}, u32[]{:S(2)}, u32[]{:S(2)}) collective-permute-start(bf16[2,112,2560]{2,1,0:T(8,128)(2,1)} %collective-permute-done.refs_3_), channel_id=1, source_target_pairs={{0,1},{1,0},{2,3},{3,2},{4,5},{5,4},{6,7},{7,6}} | collective-permute-start | bytes 3440648 | tf_op jit(solution)/shard_map/ppermute | solution.py:821
